TPU v7x, 32 devices: a whole 2x2x4 slice. The times are simulated.
32 devices in a mesh: pb: 8 (over y, x, core), ga: 4 (over z).
Axes of the slice: x: 2, y: 2, z: 4, core: 2. Of those that a mesh axis runs over, the one named last changes fastest.
Arguments:
- query_points: float32 [3, 32768], P(None, 'pb'), may hold values from 0 to 1
- cotangent: bfloat16 [64, 32768], P(None, 'pb'), may hold values from -6 to 6
- slab_ids: int32 [8, 32768], P(None, 'pb'), may hold values from -1 to 3
- rel_cells: int32 [8, 32768], P(None, 'pb'), may hold values from 0 to 511
- offsets: int32 [4, 256], P('ga', 'pb'), may hold values from 0 to 15872
- latent: bfloat16 [4, 64, 16384], P('ga', None, 'pb'), may hold values from -6 to 6
- w_in: float32 [80, 6], replicated, may hold values from -2.5 to 2.5
- b_in: float32 [80], replicated, may hold values from -3 to 3
- w_out: bfloat16 [64, 80], replicated, may hold values from -0.625 to 0.625
- b_out: float32 [64], replicated, may hold values from -3 to 3
Outputs:
- grid_grad: float32 [4, 64, 16384], P('ga', None, 'pb')
- w_in_grad: float32 [80, 6], replicated
- b_in_grad: float32 [80], replicated
- w_out_grad: float32 [64, 80], replicated
- b_out_grad: float32 [64], replicated
Inputs may be any that keep to these rules, and one draw needn't show every extreme that they name: `slab_ids`: -1 marks a padding slot; otherwise the slab that holds the neighbour cell.
All inputs are finite; a program needn't handle non-finite values.
Results may differ from a plain program's by a relative error of at most 0.0085.
Values may be sent and summed in bfloat16 or wider, within the bound.
A program may use at most 64 MiB of HBM per device.

v0:
```python
import functools
import math

import jax
import jax.numpy as jnp
from jax import lax
from jax.experimental import pallas as pl
from jax.experimental.pallas import tpu as pltpu
from jax.sharding import PartitionSpec as P

KN = 8
TILE = 128
WIN = 512
GX = 64
ZS = 4
SPAN = WIN + 128
CAP = 256
EXTRA = 16
F32 = jnp.float32
BF16 = jnp.bfloat16


def dot(a, b):
    return jnp.dot(a, b, preferred_element_type=F32)


def dot_nt(a, b):
    return lax.dot_general(a, b, (((1,), (1,)), ((), ())), preferred_element_type=F32)


def window_base(offset, cells):
    return jnp.minimum(offset // 128 * 128, cells - SPAN)


def gelu_parts(x):
    z = jnp.abs(x) * (2.0**-0.5)
    t = 1.0 / (1.0 + 0.3275911 * z)
    e = jnp.exp(-0.5 * x * x)
    poly = ((((1.061405429 * t - 1.453152027) * t + 1.421413741) * t - 0.284496736) * t + 0.254829592) * t
    tail = 0.5 * poly * e
    cdf = jnp.where(x < 0, tail, 1.0 - tail)
    return x * cdf, cdf + x * e * ((2.0 * math.pi) ** -0.5)


def prepare(tiles, cells, meta_ref, ids_ref, rel_ref, pos_ref, relp_ref):
    slab = meta_ref[tiles]
    lives = []
    for t in range(tiles):
        cols = slice(t * TILE, (t + 1) * TILE)
        lives.append(jnp.where(ids_ref[:, cols] == slab, 1.0, 0.0))
        shift = meta_ref[t] - window_base(meta_ref[t], cells) + 1
        relp_ref[t * KN : (t + 1) * KN, :] = (rel_ref[:, cols] + shift).astype(F32)
    live = jnp.concatenate(lives, 0)
    rows = tiles * KN
    packed = live.astype(BF16)
    tri = jnp.where(
        lax.broadcasted_iota(jnp.int32, (TILE, TILE), 0) < lax.broadcasted_iota(jnp.int32, (TILE, TILE), 1), 1.0, 0.0
    ).astype(BF16)
    before = dot(packed, tri)
    total = dot(packed, jnp.ones((TILE, TILE), BF16))
    r = lax.broadcasted_iota(jnp.int32, (rows, rows), 0)
    c = lax.broadcasted_iota(jnp.int32, (rows, rows), 1)
    low = jnp.where((r // KN == c // KN) & (c < r), 1.0, 0.0).astype(BF16)
    start = dot(low, total.astype(BF16))
    pos_ref[...] = jnp.where(live > 0, before + start, -1.0e6)
    most = jnp.max(start + total).astype(jnp.int32)
    return (most + CAP - 1) // CAP


def pack_tile(t, c, base, slab, data_ref, pos_ref, relp_ref):
    channels = data_ref.shape[0] - EXTRA
    rows = pl.ds(pl.multiple_of(t * KN, KN), KN)
    pos = pos_ref[rows, :] - (c * CAP).astype(F32)
    relp = relp_ref[rows, :]
    place = lax.broadcasted_iota(jnp.int32, (CAP, TILE), 0).astype(F32)
    found = jnp.zeros((CAP, TILE), F32)
    for k in range(KN):
        found = jnp.where(pos[k : k + 1, :] == place, relp[k : k + 1, :], found)
    high = found.astype(BF16)
    low = (found - high.astype(F32)).astype(BF16)
    pick = jnp.where(found > 0, 1.0, 0.0).astype(BF16)
    drawn = dot_nt(data_ref[:, pl.ds(pl.multiple_of(t * TILE, TILE), TILE)], pick)
    ones = jnp.ones((8, TILE), BF16)
    spot = (dot_nt(ones, high) + dot_nt(ones, low)).astype(jnp.int32) - 1
    cell = spot + base
    along = [cell // (GX * ZS), cell // ZS % GX, cell % ZS + slab * ZS]
    along = [(a.astype(F32) + 0.5) / GX for a in along]
    row = lax.broadcasted_iota(jnp.int32, (8, CAP), 0)
    centre = jnp.where(row < 6, jnp.where(row % 3 == 0, along[0], jnp.where(row % 3 == 1, along[1], along[2])), 0.0)
    centre = jnp.concatenate([centre, jnp.zeros((8, CAP), F32)], 0)
    inputs = jnp.concatenate([drawn[channels:], centre], 0).astype(BF16)
    onehot = jnp.where(lax.broadcasted_iota(jnp.int32, (SPAN, CAP), 0) == spot[:1, :], 1.0, 0.0).astype(BF16)
    return drawn[:channels], inputs, onehot


def forward_kernel(tiles, group, meta_ref, data_ref, ids_ref, rel_ref, w1_ref, w2_ref, out_ref, pos_ref, relp_ref, grid_ref):
    cells = grid_ref.shape[1]
    chunks = prepare(tiles, cells, meta_ref, ids_ref, rel_ref, pos_ref, relp_ref)
    slab = meta_ref[tiles]

    grid_ref[...] = jnp.zeros_like(grid_ref)

    def body(i, _):
        c, g = i // (tiles // group), i % (tiles // group)
        done = []
        for u in range(group):
            t = g * group + u
            base = window_base(meta_ref[t], cells)
            cot, inputs, onehot = pack_tile(t, c, base, slab, data_ref, pos_ref, relp_ref)
            hidden = gelu_parts(dot(w1_ref[...], inputs))[0].astype(BF16)
            kernel = dot(w2_ref[...], jnp.concatenate([hidden, inputs], 0))
            done.append((base, dot_nt((kernel * cot).astype(BF16), onehot)))
        for base, part in done:
            at = pl.ds(pl.multiple_of(base, 128), SPAN)
            grid_ref[:, at] += part
        return 0

    lax.fori_loop(0, chunks * (tiles // group), body, 0)
    owned = out_ref.shape[2]
    for p in range(out_ref.shape[0]):
        out_ref[p] = grid_ref[:, p * owned : (p + 1) * owned].astype(out_ref.dtype)


def backward_kernel(tiles, group, meta_ref, data_ref, ids_ref, rel_ref, w1_ref, w2t_ref, feats_ref, out_ref, pos_ref, relp_ref):
    cells = feats_ref.shape[1]
    chunks = prepare(tiles, cells, meta_ref, ids_ref, rel_ref, pos_ref, relp_ref)
    slab = meta_ref[tiles]

    out_ref[...] = jnp.zeros_like(out_ref)

    def body(i, _):
        c, g = i // (tiles // group), i % (tiles // group)
        sums = []
        for u in range(group):
            t = g * group + u
            base = window_base(meta_ref[t], cells)
            cot, inputs, onehot = pack_tile(t, c, base, slab, data_ref, pos_ref, relp_ref)
            hidden, slope = gelu_parts(dot(w1_ref[...], inputs))
            feats = dot(feats_ref[:, pl.ds(pl.multiple_of(base, 128), SPAN)], onehot)
            grad_kernel = (feats * cot).astype(BF16)
            grad_pre = (dot(w2t_ref[...], grad_kernel) * slope).astype(BF16)
            sums.append(
                dot_nt(
                    jnp.concatenate([grad_kernel, grad_pre], 0),
                    jnp.concatenate([hidden.astype(BF16), inputs], 0),
                )
            )
        out_ref[...] += functools.reduce(lambda a, b: a + b, sums)
        return 0

    lax.fori_loop(0, chunks * (tiles // group), body, 0)


def split(values, parts):
    pieces = []
    for _ in range(parts):
        piece = lax.reduce_precision(values, 8, 7)
        pieces.append(piece.astype(BF16))
        values = values - piece
    return pieces


def shards(query_points, cotangent, slab_ids, rel_cells, offsets, latent, w_in, b_in, w_out, b_out):
    n_pb = lax.axis_size("pb")
    channels, owned = latent.shape[1], latent.shape[2]
    hid = w_in.shape[0]
    queries_dev = query_points.shape[1]
    tiles = queries_dev // TILE
    group = math.gcd(tiles, 4)
    cells = owned * n_pb

    slab_feats = lax.all_gather(latent[0], "pb", axis=1, tiled=True)

    meta = jnp.concatenate([offsets[0], lax.axis_index("ga")[None].astype(jnp.int32)])
    p_hi, p_lo = split(query_points, 2)
    ones = jnp.ones((3, queries_dev), BF16)
    data = jnp.concatenate([cotangent, p_hi, p_lo, p_hi, ones, jnp.zeros((EXTRA - 12, queries_dev), BF16)], 0)
    w_hi, w_lo = split(w_in, 2)
    b_parts = jnp.stack(split(b_in, 3), 1)
    w1 = jnp.concatenate(
        [w_hi[:, :3], w_hi[:, :3], w_lo[:, :3], b_parts, jnp.zeros((hid, EXTRA - 12), BF16),
         w_hi[:, 3:], w_lo[:, 3:], jnp.zeros((hid, 10), BF16)], 1)
    bo_parts = jnp.stack(split(b_out, 3), 1)
    w2 = jnp.concatenate(
        [w_out, jnp.zeros((channels, 9), BF16), bo_parts, jnp.zeros((channels, EXTRA + 4), BF16)], 1)

    vmem = pl.BlockSpec(memory_space=pltpu.VMEM)
    smem = pl.BlockSpec(memory_space=pltpu.SMEM)
    scratch = [pltpu.VMEM((tiles * KN, TILE), F32), pltpu.VMEM((tiles * KN, TILE), F32)]
    partial_grad = pl.pallas_call(
        functools.partial(forward_kernel, tiles, group),
        out_shape=jax.ShapeDtypeStruct((n_pb, channels, owned), BF16),
        in_specs=[smem] + [vmem] * 5,
        out_specs=vmem,
        scratch_shapes=scratch + [pltpu.VMEM((channels, cells), F32)],
        cost_estimate=pl.CostEstimate(flops=10**10, bytes_accessed=10**7, transcendentals=0),
        compiler_params=pltpu.CompilerParams(vmem_limit_bytes=40 * 2**20),
        name="forward",
    )(meta, data, slab_ids, rel_cells, w1, w2)
    partial_grad, slab_feats = lax.optimization_barrier((partial_grad, slab_feats))
    received = lax.psum_scatter(partial_grad, "pb", scatter_dimension=0, tiled=True)
    sums = pl.pallas_call(
        functools.partial(backward_kernel, tiles, group),
        out_shape=jax.ShapeDtypeStruct((channels + hid, hid + EXTRA + 16), F32),
        in_specs=[smem] + [vmem] * 6,
        out_specs=vmem,
        scratch_shapes=scratch,
        cost_estimate=pl.CostEstimate(flops=10**10, bytes_accessed=10**7, transcendentals=0),
        compiler_params=pltpu.CompilerParams(vmem_limit_bytes=40 * 2**20),
        name="backward",
    )(meta, data, slab_ids, rel_cells, w1, w_out.T, slab_feats)
    scale = float(queries_dev * n_pb) ** (-0.5)
    sums = jnp.sum(lax.all_gather(sums, "ga", axis=0), 0)
    sums = jnp.sum(lax.all_gather(sums, "pb", axis=0), 0) * scale
    low = sums[channels:, hid:]
    w_in_grad = jnp.concatenate([low[:, 0:3] + low[:, 3:6], low[:, EXTRA : EXTRA + 3]], 1)
    return (
        received.astype(F32),
        w_in_grad,
        low[:, 9],
        sums[:channels, :hid],
        sums[:channels, hid + 9],
    )


def solution(mesh):
    return jax.shard_map(
        shards,
        mesh=mesh,
        in_specs=(
            P(None, "pb"),
            P(None, "pb"),
            P(None, "pb"),
            P(None, "pb"),
            P("ga", "pb"),
            P("ga", None, "pb"),
            P(),
            P(),
            P(),
            P(),
        ),
        out_specs=(P("ga", None, "pb"), P(), P(), P(), P()),
        check_vma=False,
    )
```

profile of v0, /device:TPU:0, one launch (start us, length us, event | category | flops | bytes accessed | tf_op | source)
XLA Modules:
  0.0 97.9 jit_solution(4621845075091505745)
XLA Ops:
  7.2 0.0 copy-start.4
  7.2 0.0 copy-start.2
  7.2 0.0 copy-start.1
  7.2 0.0 all-gather.5.cloned.1.call-start
  7.2 0.7 all-gather.5.cloned.1.call-update
  7.9 0.0 reduce-scatter.2.cloned.1.call-start
  8.0 0.7 fusion.8
  8.6 0.7 fusion.3
  9.4 0.3 concatenate.17
  9.6 0.1 copy.45.w1_ref
  9.8 0.7 fusion.13
  10.4 0.1 copy.44
  10.5 0.1 copy.43
  10.6 0.1 copy.42
  10.8 0.9 fusion.1
  11.7 2.2 %concatenate.16.data_ref = bf16[80,4096]{1,0:T(8,128)(2,1)S(1)} concatenate(bf16[64,4096]{1,0:T(8,128)(2,1)} %param.11, bf16[3,4096]{1,0:T(4,128)(2,1)S(1)} %get-tuple-element.27, bf16[3,4096]{1,0:T(4,128)(2,1)S(1)} %get-tuple-element.26, bf16[3,4096]{1,0:T(4,128)(2,1)S(1)} %get-tuple-element.27, bf16[3,4096]{1,0:T(4,128)(2,1)S(1)} %broadcast_in_dim.22, ...), dimensions={0} | concatenate | bytes 1310720 | tf_op jit(solution)/shard_map/concatenate | solution.py:177
  13.9 0.8 concatenate.18.w2_ref
  14.7 0.0 copy-done.4
  14.8 0.1 pad_add_fusion.meta_ref
  14.8 0.0 copy-done.2
  14.8 0.0 copy-done.1
  14.8 22.6 %forward.1 = bf16[8,64,2048]{2,1,0:T(8,128)(2,1)} custom-call(s32[33]{0:T(128)S(1)} %pad_add_fusion.meta_ref, bf16[80,4096]{1,0:T(8,128)(2,1)S(1)} %concatenate.16.data_ref, s32[8,4096]{1,0:T(8,128)S(1)} %copy-done.1, s32[8,4096]{1,0:T(8,128)S(1)} %copy-done.2, bf16[80,32]{1,0:T(8,128)(2,1)S(1)} %copy.45.w1_ref, bf16[64,112]{1,0:T(8,128)(2,1)S(1)} %concatenate.18.w2_ref), custom_call_target="tpu_custom_call" | custom-call | flops 10000000000 | bytes 10000000 | tf_op jit(solution)/shard_map/forward/pallas_call | solution.py:190
  37.4 0.0 copy-start.3
  37.4 3.1 %all-gather.5.cloned.1.call-done = bf16[1,64,16384]{2,1,0:T(8,128)(2,1)} async-done(((bf16[1,64,2048]{2,1,0:T(8,128)(2,1)}), bf16[1,64,16384]{2,1,0:T(8,128)(2,1)}) %all-gather.5.cloned.1.call-update) | async-done | bytes 2097168 | tf_op jit(solution)/shard_map/all_gather | solution.py:172
  40.5 0.0 copy-start
  40.5 0.0 reduce-scatter.2.cloned.1.call-update
  40.5 0.0 copy-done.3
  40.5 0.1 copy.46
  40.6 1.5 %copy-done = bf16[1,64,16384]{2,1,0:T(8,128)(2,1)S(1)} copy-done((bf16[1,64,16384]{2,1,0:T(8,128)(2,1)S(1)}, bf16[1,64,16384]{2,1,0:T(8,128)(2,1)}, u32[]{:S(2)}) %copy-start) | copy-done | bytes 2097176
  42.1 19.4 %backward.1 = f32[144,112]{1,0:T(8,128)S(1)} custom-call(s32[33]{0:T(128)S(1)} %pad_add_fusion.meta_ref, bf16[80,4096]{1,0:T(8,128)(2,1)S(1)} %concatenate.16.data_ref, s32[8,4096]{1,0:T(8,128)S(1)} %copy-done.1, s32[8,4096]{1,0:T(8,128)S(1)} %copy-done.2, bf16[80,32]{1,0:T(8,128)(2,1)S(1)} %copy.45.w1_ref, bf16[80,64]{1,0:T(8,128)(2,1)S(1)} %bitcast.18, ...), custom_call_target="tpu_custom_call" | custom-call | flops 10000000000 | bytes 10000000 | tf_op jit(solution)/shard_map/backward/pallas_call | solution.py:202
  61.5 14.0 %all-gather.1 = f32[576,112]{1,0:T(8,128)S(1)} all-gather(f32[144,112]{1,0:T(8,128)S(1)} %backward.1), channel_id=3, replica_groups=mesh['pb'=8,'ga'=4] {'ga'}, dimensions={0}, use_global_device_ids=true | all-gather | bytes 322560 | tf_op jit(solution)/shard_map/all_gather | solution.py:213
  75.5 10.8 %all-gather.2 = f32[1152,112]{1,0:T(8,128)S(1)} all-gather(f32[144,112]{1,0:T(8,128)S(1)} %reduce_sum.18), channel_id=4, replica_groups=mesh['pb'=8,'ga'=4] {'pb'}, dimensions={0}, use_global_device_ids=true | all-gather | bytes 580608 | tf_op jit(solution)/shard_map/all_gather | solution.py:214
  86.4 0.6 slice.50
  87.0 0.1 slice_add_fusion
  87.1 0.1 copy.48
  87.2 0.1 copy.49
  87.2 0.6 pad_maximum_fusion
  87.9 0.7 slice_reduce_fusion.1
  88.6 0.7 slice_reduce_fusion
  89.3 0.0 reduce-scatter.2.cloned.1.call-done
  89.3 1.8 %convert_element_type.43 = f32[1,64,2048]{2,1,0:T(8,128)} convert(bf16[1,64,2048]{2,1,0:T(8,128)(2,1)} %reduce-scatter.2.cloned.1.call-done) | non-fusion elementwise | flops 131072 | bytes 786432 | tf_op jit(solution)/shard_map/convert_element_type | solution.py:218
  (10 shorter events, 0.1 us)
Async XLA Ops:
  7.2 7.6 %copy-start.4 = (s32[1,32]{1,0:T(1,128)S(1)}, s32[1,32]{1,0:T(1,128)}, u32[]{:S(2)}) copy-start(s32[1,32]{1,0:T(1,128)} %param.14) | copy-start | bytes 388
  7.2 7.7 %copy-start.2 = (s32[8,4096]{1,0:T(8,128)S(1)}, s32[8,4096]{1,0:T(8,128)}, u32[]{:S(2)}) copy-start(s32[8,4096]{1,0:T(8,128)} %rel_ref.3) | copy-start | bytes 393220
  7.2 7.6 %copy-start.1 = (s32[8,4096]{1,0:T(8,128)S(1)}, s32[8,4096]{1,0:T(8,128)}, u32[]{:S(2)}) copy-start(s32[8,4096]{1,0:T(8,128)} %ids_ref.3) | copy-start | bytes 393220
  7.2 33.3 %all-gather.5.cloned.1.call-start = ((), (), s32[]{:S(2)}) async-start(), calls=%async_computation.2 | async-start | bytes 2359296 | tf_op jit(solution)/shard_map/all_gather | solution.py:172
  7.9 81.3 %reduce-scatter.2.cloned.1.call-start = ((), (), s32[]{:S(2)}) async-start(), calls=%async_computation.1 | async-start | bytes 2359296 | tf_op jit(solution)/shard_map/reduce_scatter | solution.py:201
  37.4 3.1 %copy-start.3 = (bf16[64,80]{1,0:T(8,128)(2,1)S(1)}, bf16[64,80]{1,0:T(8,128)(2,1)}, u32[]{:S(2)}) copy-start(bf16[64,80]{1,0:T(8,128)(2,1)} %param.18) | copy-start | bytes 30724
  40.5 1.6 %copy-start = (bf16[1,64,16384]{2,1,0:T(8,128)(2,1)S(1)}, bf16[1,64,16384]{2,1,0:T(8,128)(2,1)}, u32[]{:S(2)}) copy-start(bf16[1,64,16384]{2,1,0:T(8,128)(2,1)} %all-gather.5.cloned.1.call-done) | copy-start | bytes 6291460
Sparse Core Ops, SparseCore 0:
  9.9 30.5 all-gather.4
  43.8 42.1 reduce-scatter.1
where the time goes:
time: 98.3 us; the launch traced here: 97.9 us
  Pallas kernels  42 us (43%)
  blocking collectives  24.8 us (25%)
  between operations  14.2 us (14%)
  local copies, waits for them, and re-layouts  7.52 us (8%)
  other arithmetic  5.54 us (6%)
  waiting for transfers between devices  3.75 us (4%)
    pallas_call x1, Pallas kernels, shards(): pl.pallas_call(functools.partial(forward_kernel, tiles, group), out_shape...  22.6 us
    pallas_call x1, Pallas kernels, shards(): pl.pallas_call(functools.partial(backward_kernel, tiles, group), out_shap...  19.4 us
    all_gather x1, blocking collectives, shards(): sums = jnp.sum(lax.all_gather(sums, 'ga', axis=0), 0)  14 us
    all_gather x1, blocking collectives, shards(): sums = jnp.sum(lax.all_gather(sums, 'pb', axis=0), 0) * scale  10.8 us
    all_gather x1, waiting for transfers between devices, shards(): slab_feats = lax.all_gather(latent[0], 'pb', axis=1, tiled=True)  3.05 us
    concatenate x1, local copies, waits for them, and re-layouts, shards(): jnp.concatenate([cotangent, p_hi, p_lo, p_hi, ones, jnp.zeros((EXTRA - 12...  2.22 us
  transfers between devices with their start and end apart: 2, of which 1 were waited for; matrix products, arithmetic and copies ran while one was open for 10% of the time, Pallas kernels for 43%

commit v1 on v0

v1 whole, which is shorter than its diff:
```python
import functools
import math

import jax
import jax.numpy as jnp
from jax import lax
from jax.experimental import pallas as pl
from jax.experimental.pallas import tpu as pltpu
from jax.sharding import PartitionSpec as P

KN = 8
TILE = 128
WIN = 512
GX = 64
ZS = 4
LANES = 128
SPAN = WIN // LANES + 1
CAP = 256
XR = 48
F32 = jnp.float32
BF16 = jnp.bfloat16
I32 = jnp.int32
MESH = pl.DeviceIdType.MESH
HIGHEST = lax.Precision.HIGHEST


def dot(a, b):
    return jnp.dot(a, b, preferred_element_type=F32)


def dot_nt(a, b):
    return lax.dot_general(a, b, (((1,), (1,)), ((), ())), preferred_element_type=F32)


def exact(a, b):
    return jnp.dot(a, b, preferred_element_type=F32, precision=HIGHEST)


def exact_nt(a, b):
    return lax.dot_general(a, b, (((1,), (1,)), ((), ())), preferred_element_type=F32, precision=HIGHEST)


def rows_of(shape):
    return lax.broadcasted_iota(I32, shape, 0)


def cols_of(shape):
    return lax.broadcasted_iota(I32, shape, 1)


def gelu_parts(x):
    z = jnp.abs(x) * (2.0**-0.5)
    t = 1.0 / (1.0 + 0.3275911 * z)
    e = jnp.exp(-0.5 * x * x)
    poly = ((((1.061405429 * t - 1.453152027) * t + 1.421413741) * t - 0.284496736) * t + 0.254829592) * t
    tail = 0.5 * poly * e
    cdf = jnp.where(x < 0, tail, 1.0 - tail)
    return x * cdf, cdf + x * e * ((2.0 * math.pi) ** -0.5)


def mask_of(cond):
    return jnp.where(cond, 1.0, 0.0).astype(BF16)


def split3(v):
    a = v.astype(BF16)
    r = v - a.astype(F32)
    b = r.astype(BF16)
    return a, b, (r - b.astype(F32)).astype(BF16)


def weights(win_ref, bin_ref, wout_ref, bout_ref, pad_ref, w1_ref, w2_ref, w2t_ref):
    hid, channels = win_ref.shape[0], wout_ref.shape[0]
    pad_ref[...] = jnp.zeros_like(pad_ref)
    pad_ref[:hid, : win_ref.shape[1]] = win_ref[...]
    wide = pad_ref[:hid, :]
    w_hi = wide.astype(BF16)
    w_lo = (wide - w_hi.astype(F32)).astype(BF16)
    k, col = rows_of((LANES, LANES)), cols_of((LANES, LANES))
    s_hi = mask_of(((k < 3) & ((col == k) | (col == k + 8))) | ((k >= 3) & (k < 6) & (col == k + 13)))
    s_lo = mask_of(((k < 3) & (col == k + 24)) | ((k >= 3) & (k < 6) & (col == k + 29)))
    w1 = dot(w_hi, s_hi) + dot(w_lo, s_lo)
    pad_ref[0:1, :hid] = bin_ref[...]
    diag = jnp.where(rows_of((hid, LANES)) == cols_of((hid, LANES)), pad_ref[0:1, :], 0.0)
    for i, part in enumerate(split3(diag)):
        w1 += dot(part, mask_of(col == 3 + i))
    w1_ref[...] = w1.astype(BF16)

    pad_ref[0:channels, :hid] = wout_ref[...].astype(F32)
    pad_ref[0:channels, hid:] = jnp.zeros((channels, LANES - hid), F32)
    w_out = pad_ref[0:channels, :].astype(BF16)
    w2 = dot(w_out, mask_of(k == col))
    eye = mask_of(rows_of((hid, LANES)) == cols_of((hid, LANES)))
    w2t_ref[...] = dot_nt(eye, w_out).astype(BF16)
    pad_ref[0:1, :channels] = bout_ref[...]
    diag = jnp.where(rows_of((channels, LANES)) == cols_of((channels, LANES)), pad_ref[0:1, :], 0.0)
    for i, part in enumerate(split3(diag)):
        w2 += dot(part, mask_of(col == hid + 3 + i))
    w2_ref[...] = w2.astype(BF16)


def order_parts(tiles, limit, offv_ref, table_ref):
    pairs = SPAN * tiles
    lanes = -(-pairs // LANES) * LANES
    base_row = jnp.minimum(lax.shift_right_logical(offv_ref[...], 7), limit)
    wide = jnp.concatenate([base_row, jnp.zeros((1, LANES - tiles), I32)], 1)
    pick = rows_of((tiles, LANES)) == cols_of((tiles, LANES))
    column = jnp.sum(jnp.where(pick, wide.astype(F32), 0.0), 1, keepdims=True)
    key = jnp.concatenate([column + float(j) for j in range(SPAN)], 0)
    key = jnp.broadcast_to(key, (pairs, lanes))
    p, q = rows_of((pairs, lanes)), cols_of((pairs, lanes))
    key_row = jnp.sum(jnp.where(p == q, key, 0.0), 0, keepdims=True)
    key_row = jnp.where(q[:1] < pairs, key_row, 1.0e6)
    ahead = (key_row == key) & (q < p)
    rank = jnp.sum(jnp.where((key_row < key) | ahead, 1.0, 0.0), 1, keepdims=True)
    again = jnp.sum(jnp.where(ahead, 1.0, 0.0), 1, keepdims=True)
    here = rank == q.astype(F32)
    order = jnp.sum(jnp.where(here, p.astype(F32), 0.0), 0, keepdims=True)
    keep = jnp.sum(jnp.where(here & (again > 0), 1.0, 0.0), 0, keepdims=True)
    upto = jnp.sum(jnp.where(key <= q.astype(F32), 1.0, 0.0), 0, keepdims=True)
    some = jnp.sum(jnp.where(key == q.astype(F32), 1.0, 0.0), 0, keepdims=True)
    some = jnp.minimum(some, 1.0)
    last = jnp.maximum(upto - 1.0, 0.0)
    rows = jnp.concatenate([order, keep, last, some, jnp.zeros((4, lanes), F32)], 0)
    table_ref[...] = rows.astype(I32)


def kernel(
    n_pb, n_ga, scale,
    step_ref, offs_ref, offv_ref, qp_ref, cot_ref, ids_ref, rel_ref, latent_ref, win_ref, bin_ref, wout_ref, bout_ref,
    grid_ref, gwin_ref, gbin_ref, gwout_ref, gbout_ref, more_ref,
    pts_ref, pos_ref, from_ref, upto_ref, pad_ref, w1_ref, w2_ref, w2t_ref, tablev_ref, table_ref,
    cots_ref, hid_ref, slope_ref, x_ref, spot_ref, parts_ref, sums_ref, feats_ref,
    near_ref, nearin_ref, far_ref, farin_ref, own_ref, acc_ref,
    ar_ref, arin_ref, gaall_ref, fin_ref,
    table_sem, gsend, grecv, fsend, nsend, nrecv, rsend, rrecv, asend, arecv, bsend, brecv, csend, crecv,
):
    me, slab = lax.axis_index("pb"), lax.axis_index("ga")
    chips = n_pb // 2
    chip, core = me // 2, me % 2
    sibling = chip * 2 + 1 - core
    tiles = cot_ref.shape[1] // TILE
    channels, hid = cot_ref.shape[0], win_ref.shape[0]
    blocks = latent_ref.shape[2] // LANES
    limit = blocks * n_pb - SPAN
    group = math.gcd(tiles, 4)

    def send(src, dst, ssem, rsem, where):
        return pltpu.make_async_remote_copy(
            src_ref=src, dst_ref=dst, send_sem=ssem, recv_sem=rsem, device_id=where, device_id_type=MESH
        )

    def peer(m):
        return lax.rem(chip + m, chips) * 2 + core

    def peer_back(m):
        return lax.rem(chip + chips - m, chips) * 2 + core

    barrier = pltpu.get_barrier_semaphore()
    for m in range(1, n_pb):
        pl.semaphore_signal(barrier, inc=1, device_id={"pb": lax.rem(me + m, n_pb)}, device_id_type=MESH)
    for m in range(1, n_ga):
        pl.semaphore_signal(barrier, inc=1, device_id={"ga": lax.rem(slab + m, n_ga)}, device_id_type=MESH)

    mine = me * blocks
    for b in range(blocks):
        feats_ref[mine + b] = latent_ref[0, :, b * LANES : (b + 1) * LANES]
    pts_ref[...] = jnp.ones_like(pts_ref)
    pts_ref[0:3, :] = qp_ref[...]
    order_parts(tiles, limit, offv_ref, tablev_ref)
    weights(win_ref, bin_ref, wout_ref, bout_ref, pad_ref, w1_ref, w2_ref, w2t_ref)

    pl.semaphore_wait(barrier, n_pb - 1 + n_ga - 1)

    def feats_of(d):
        return feats_ref.at[pl.ds(d * blocks, blocks)]

    out = []
    for m in range(1, chips):
        out.append(send(feats_of(me), feats_of(me), gsend.at[m], grecv.at[me], {"pb": peer(m)}))
    out.append(send(feats_of(me), feats_of(me), gsend.at[0], grecv.at[me], {"pb": sibling}))
    for copy in out:
        copy.start()
    table_copy = pltpu.make_async_copy(tablev_ref, table_ref, table_sem)
    table_copy.start()

    lives = [jnp.where(ids_ref[:, t * TILE : (t + 1) * TILE] == slab, 1.0, 0.0) for t in range(tiles)]
    live = jnp.concatenate(lives, 0)
    rows = tiles * KN
    packed = live.astype(BF16)
    before = dot(packed, mask_of(rows_of((TILE, TILE)) < cols_of((TILE, TILE))))
    total = dot(packed, jnp.ones((TILE, TILE), BF16))
    r, c = rows_of((rows, rows)), cols_of((rows, rows))
    start = dot(mask_of((r // KN == c // KN) & (c < r)), total.astype(BF16))
    skip = (step_ref[0] * CAP).astype(F32)
    pos_ref[...] = jnp.where(live > 0, before + start - skip, -1.0e6)
    from_ref[...] = start - skip
    upto_ref[...] = start + total - skip
    left = jnp.max(start + total - skip - float(CAP), axis=0, keepdims=True)
    left = jnp.max(left, axis=1, keepdims=True)

    def tile_base(t):
        return jnp.minimum(lax.shift_right_logical(offs_ref[0, t], 7), limit)

    def query_side(t):
        cols = pl.ds(pl.multiple_of(t * TILE, TILE), TILE)
        lines = pl.ds(pl.multiple_of(t * KN, KN), KN)
        base = tile_base(t)
        pos = pos_ref[lines, :].astype(BF16)
        place = rows_of((CAP, TILE)).astype(F32).astype(BF16)
        pick = jnp.zeros((CAP, TILE), BF16)
        one = jnp.ones((CAP, TILE), BF16)
        for k in range(KN):
            pick = jnp.where(pos[k : k + 1, :] == place, one, pick)
        relp = rel_ref[:, cols] + (offs_ref[0, t] - base * LANES)
        low = (relp & (LANES - 1)).astype(F32)
        high = lax.shift_right_logical(relp, 7).astype(F32)
        points = pts_ref[:, cols]
        p_hi = points.astype(BF16).astype(F32)
        small = jnp.concatenate([p_hi, points - p_hi, low, high], 0).astype(BF16)
        data = jnp.concatenate([cot_ref[:, cols], small], 0)
        drawn = dot_nt(data, pick)
        cot = drawn[:channels]
        head = drawn[channels : channels + 16]
        wide_from = jnp.concatenate([from_ref[lines, :]] * (CAP // TILE), 1)
        wide_upto = jnp.concatenate([upto_ref[lines, :]] * (CAP // TILE), 1)
        index = cols_of((KN, CAP)).astype(F32)
        which = (index >= wide_from) & (index < wide_upto)
        lo = jnp.sum(jnp.where(which, drawn[channels + 16 : channels + 24], 0.0), 0, keepdims=True)
        hi = jnp.sum(jnp.where(which, drawn[channels + 24 : channels + 32], 0.0), 0, keepdims=True)
        lo = jnp.broadcast_to(lo, (8, CAP))
        hi = jnp.broadcast_to(hi, (8, CAP))
        cell = (base + hi.astype(I32)) * LANES + lo.astype(I32)
        row = rows_of((8, CAP))
        along = jnp.where(
            row == 0,
            lax.shift_right_logical(cell, int(math.log2(GX * ZS))),
            jnp.where(
                row == 1,
                lax.shift_right_logical(cell, int(math.log2(ZS))) & (GX - 1),
                (cell & (ZS - 1)) + slab * ZS,
            ),
        )
        centre = jnp.where(row < 3, (along.astype(F32) + 0.5) / GX, 0.0)
        x = jnp.concatenate([head, centre, head[:8], centre, jnp.zeros((8, CAP), F32)], 0).astype(BF16)
        hidden, slope = gelu_parts(dot(w1_ref[:, :XR], x))
        hidden = hidden.astype(BF16)
        kern = dot(w2_ref[...], jnp.concatenate([hidden, x], 0))
        grad = (kern * cot).astype(BF16)
        part = dot_nt(spread(hi, grad), lane_onehot(lo))
        return cot.astype(BF16), hidden, slope, x, jnp.where(row < 4, lo, hi), part

    def lane_onehot(lo):
        row = jnp.broadcast_to(lo[:1], (LANES, CAP)).astype(BF16)
        return jnp.where(
            rows_of((LANES, CAP)).astype(F32).astype(BF16) == row, jnp.ones((LANES, CAP), BF16), jnp.zeros((LANES, CAP), BF16)
        )

    def spread(hi, grad):
        full = jnp.concatenate([hi, hi], 0)
        pieces = []
        for j in range(SPAN):
            on = jnp.where(full == float(j), 1.0, 0.0).astype(BF16)
            pieces.append(grad * jnp.concatenate([on] * (channels // 16), 0))
        return jnp.concatenate(pieces, 0)

    def first(i, carry):
        done = [(i * group + u, query_side(i * group + u)) for u in range(group)]
        for t, (cot, hidden, slope, x, spot, part) in done:
            cots_ref[t] = cot
            hid_ref[t] = hidden
            slope_ref[t] = slope
            x_ref[t] = x
            spot_ref[t] = spot
            for j in range(SPAN):
                parts_ref[j * tiles + t] = part[j * channels : (j + 1) * channels]
        return carry

    lax.fori_loop(0, tiles // group, first, 0)

    table_copy.wait()

    def pair_at(line, b):
        return jnp.clip(table_ref[line, b], 0, SPAN * tiles - 1)

    def run(i, acc):
        for u in range(group):
            at = i * group + u
            acc = acc * table_ref[1, at].astype(F32) + parts_ref[pair_at(0, at)]
            sums_ref[at] = acc
        return acc

    lax.fori_loop(0, SPAN * tiles // group, run, jnp.zeros((channels, LANES), F32))

    def block(b):
        return sums_ref[pair_at(2, b)] * table_ref[3, b].astype(F32)

    def near_copy(m):
        return send(near_ref.at[m], nearin_ref.at[m], nsend.at[m], nrecv.at[m], {"pb": sibling})

    pair = math.gcd(blocks, 4)
    order = [m % chips for m in range(1, chips + 1)]
    for i, m in enumerate(order):
        owner = lax.rem(chip + m, chips) * 2 + 1 - core

        def fill(b, carry, m=m, owner=owner):
            for u in range(pair):
                near_ref[m, b * pair + u] = block(owner * blocks + b * pair + u).astype(BF16)
            return carry

        lax.fori_loop(0, blocks // pair, fill, 0)
        if i > 0:
            near_copy(order[i - 1]).start()
    forwards = []
    for m in range(1, chips):
        d = peer_back(m)
        send(feats_of(d), feats_of(d), gsend.at[m], grecv.at[d], {"pb": d}).wait_recv()
        copy = send(feats_of(d), feats_of(d), fsend.at[m - 1], grecv.at[d], {"pb": sibling})
        copy.start()
        forwards.append(copy)
        if m == 1:
            near_copy(order[-1]).start()

    def far_copy(m):
        return send(far_ref.at[m - 1], farin_ref.at[m - 1], rsend.at[m - 1], rrecv.at[m - 1], {"pb": peer(m)})

    for i, m in enumerate(order):
        owner = lax.rem(chip + m, chips) * 2 + core
        near_copy(m).wait_recv()

        def join(b, carry, m=m, owner=owner):
            for u in range(pair):
                at = b * pair + u
                value = block(owner * blocks + at) + nearin_ref[m, at].astype(F32)
                if m:
                    far_ref[m - 1, at] = value.astype(BF16)
                else:
                    own_ref[at] = value
            return carry

        lax.fori_loop(0, blocks // pair, join, 0)
        if i > 0:
            far_copy(order[i - 1]).start()

    for m in range(chips):
        d = lax.rem(chip + m, chips) * 2 + 1 - core
        send(feats_of(d), feats_of(d), gsend.at[0], grecv.at[d], {"pb": sibling}).wait_recv()

    acc_ref[...] = jnp.zeros_like(acc_ref)

    def feature_side(t):
        spot = spot_ref[t]
        hi = jnp.broadcast_to(spot[4:5], (8, CAP))
        window = feats_ref[pl.ds(tile_base(t), SPAN)].reshape(SPAN * channels, LANES)
        drawn = dot(window, lane_onehot(spot))
        tall = jnp.concatenate([hi] * (channels // 8), 0)
        feats = drawn[:channels]
        for j in range(1, SPAN):
            feats = jnp.where(tall == float(j), drawn[j * channels : (j + 1) * channels], feats)
        grad_kernel = (feats * cots_ref[t].astype(F32)).astype(BF16)
        grad_pre = (dot(w2t_ref[...], grad_kernel) * slope_ref[t]).astype(BF16)
        return dot_nt(jnp.concatenate([grad_kernel, grad_pre], 0), jnp.concatenate([hid_ref[t], x_ref[t]], 0))

    def second(i, carry):
        acc_ref[...] += functools.reduce(lambda a, b: a + b, [feature_side(i * group + u) for u in range(group)])
        return carry

    lax.fori_loop(0, tiles // group, second, 0)

    k, l = rows_of((LANES, LANES)), cols_of((LANES, LANES))

    def gathered(shift):
        a = (l - shift >= 0) & (l - shift < 4) & ((k == hid + l - shift) | ((k == hid + 8 + l - shift) & (l - shift < 3)))
        b = (l - shift >= 4) & (l - shift < 7) & (k == hid + 16 + l - shift - 4)
        return jnp.where(a | b, 1.0, 0.0)

    top = jnp.where(cols_of((channels, LANES)) < 112, acc_ref[:channels], 0.0)
    tail = hid - channels
    top += exact(acc_ref[channels : 2 * channels], gathered(112))
    rest = exact(acc_ref[2 * channels : 2 * channels + tail], gathered(120))
    flag = jnp.where(left > 0, 1.0, 0.0)
    corner = (rows_of((tail, LANES)) == 0) & (cols_of((tail, LANES)) == 119)
    rest = jnp.where(corner, flag, rest)
    top = jnp.concatenate([top[:tail] + rest, top[tail:]], 0)
    slices = channels // n_pb
    ar_ref[...] = top.reshape(n_pb, slices, LANES)
    arin_ref[pl.ds(me, 1)] = ar_ref[pl.ds(me, 1)]
    first_hop = []
    for m in range(1, n_pb):
        to = lax.rem(me + m, n_pb)
        copy = send(ar_ref.at[to], arin_ref.at[me], asend.at[m - 1], arecv.at[me], {"pb": to})
        copy.start()
        first_hop.append(copy)
    for m in range(1, n_pb):
        d = lax.rem(me + m, n_pb)
        send(ar_ref.at[d], arin_ref.at[d], asend.at[m - 1], arecv.at[d], {"pb": d}).wait_recv()
    gaall_ref[pl.ds(slab, 1)] = jnp.sum(arin_ref[...], 0, keepdims=True)
    second_hop = []
    for m in range(1, n_ga):
        to = lax.rem(slab + m, n_ga)
        copy = send(gaall_ref.at[slab], gaall_ref.at[slab], bsend.at[m - 1], brecv.at[slab], {"ga": to})
        copy.start()
        second_hop.append(copy)
    for m in range(1, n_ga):
        d = lax.rem(slab + m, n_ga)
        send(gaall_ref.at[d], gaall_ref.at[d], bsend.at[m - 1], brecv.at[d], {"ga": d}).wait_recv()
    fin_ref[pl.ds(me, 1)] = jnp.sum(gaall_ref[...], 0, keepdims=True)
    third_hop = []
    for m in range(1, n_pb):
        to = lax.rem(me + m, n_pb)
        copy = send(fin_ref.at[me], fin_ref.at[me], csend.at[m - 1], crecv.at[me], {"pb": to})
        copy.start()
        third_hop.append(copy)

    for m in range(1, chips):
        far_copy(m).wait_recv()
    for b in range(blocks):
        value = own_ref[b]
        for m in range(1, chips):
            value += farin_ref[m - 1, b].astype(F32)
        grid_ref[0, :, b * LANES : (b + 1) * LANES] = value

    for m in range(1, n_pb):
        d = lax.rem(me + m, n_pb)
        send(fin_ref.at[d], fin_ref.at[d], csend.at[m - 1], crecv.at[d], {"pb": d}).wait_recv()
    final = fin_ref[...].reshape(channels, LANES)
    gwout_ref[...] = final[:, :hid] * scale
    more_ref[...] = jnp.broadcast_to(final[0:1, :], more_ref.shape)

    def chosen(shift):
        return jnp.where(((l < 3) & (k == shift + l)) | ((l >= 3) & (l < 6) & (k == shift + 1 + l)) | ((l == 6) & (k == shift + 3)), scale, 0.0)

    taken = jnp.concatenate([exact(final, chosen(112)), exact(final[:tail], chosen(120))], 0)
    gwin_ref[...] = taken[:, : gwin_ref.shape[1]]
    pick6 = jnp.where(cols_of((8, LANES)) == 6, 1.0, 0.0)
    gbin_ref[...] = exact_nt(pick6, taken)[0:1]
    pickb = jnp.where(cols_of((8, LANES)) == hid + 3, scale, 0.0)
    gbout_ref[...] = exact_nt(pickb, final)[0:1]

    for copy in out + forwards + first_hop + second_hop + third_hop:
        copy.wait_send()
    for m in range(chips):
        near_copy(m).wait_send()
    for m in range(1, chips):
        far_copy(m).wait_send()


def call(step, collective_id, query_points, cotangent, slab_ids, rel_cells, offsets, latent, w_in, b_in, w_out, b_out):
    n_pb, n_ga = lax.axis_size("pb"), lax.axis_size("ga")
    channels, owned = latent.shape[1], latent.shape[2]
    hid = w_in.shape[0]
    queries = query_points.shape[1]
    tiles = queries // TILE
    chips = n_pb // 2
    blocks = owned // LANES
    pairs = SPAN * tiles
    lanes = -(-pairs // LANES) * LANES
    vmem = pl.BlockSpec(memory_space=pltpu.VMEM)
    smem = pl.BlockSpec(memory_space=pltpu.SMEM)
    dma = pltpu.SemaphoreType.DMA
    slices = channels // n_pb
    return pl.pallas_call(
        functools.partial(kernel, n_pb, n_ga, float(queries * n_pb) ** (-0.5)),
        out_shape=[
            jax.ShapeDtypeStruct((1, channels, owned), F32),
            jax.ShapeDtypeStruct(w_in.shape, F32),
            jax.ShapeDtypeStruct((1, hid), F32),
            jax.ShapeDtypeStruct(w_out.shape, F32),
            jax.ShapeDtypeStruct((1, channels), F32),
            jax.ShapeDtypeStruct((8, LANES), F32),
        ],
        in_specs=[smem, smem] + [vmem] * 10,
        out_specs=[vmem] * 6,
        scratch_shapes=[
            pltpu.VMEM((8, queries), F32),
            pltpu.VMEM((tiles * KN, TILE), F32),
            pltpu.VMEM((tiles * KN, TILE), F32),
            pltpu.VMEM((tiles * KN, TILE), F32),
            pltpu.VMEM((LANES, LANES), F32),
            pltpu.VMEM((hid, LANES), BF16),
            pltpu.VMEM((channels, LANES), BF16),
            pltpu.VMEM((hid, channels), BF16),
            pltpu.VMEM((8, lanes), I32),
            pltpu.SMEM((8, lanes), I32),
            pltpu.VMEM((tiles, channels, CAP), BF16),
            pltpu.VMEM((tiles, hid, CAP), BF16),
            pltpu.VMEM((tiles, hid, CAP), F32),
            pltpu.VMEM((tiles, XR, CAP), BF16),
            pltpu.VMEM((tiles, 8, CAP), F32),
            pltpu.VMEM((pairs, channels, LANES), F32),
            pltpu.VMEM((pairs, channels, LANES), F32),
            pltpu.VMEM((n_pb * blocks, channels, LANES), BF16),
            pltpu.VMEM((chips, blocks, channels, LANES), BF16),
            pltpu.VMEM((chips, blocks, channels, LANES), BF16),
            pltpu.VMEM((chips - 1, blocks, channels, LANES), BF16),
            pltpu.VMEM((chips - 1, blocks, channels, LANES), BF16),
            pltpu.VMEM((blocks, channels, LANES), F32),
            pltpu.VMEM((channels + hid, LANES), F32),
            pltpu.VMEM((n_pb, slices, LANES), F32),
            pltpu.VMEM((n_pb, slices, LANES), F32),
            pltpu.VMEM((n_ga, slices, LANES), F32),
            pltpu.VMEM((n_pb, slices, LANES), F32),
            dma,
            dma((chips,)),
            dma((n_pb,)),
            dma((chips,)),
            dma((chips,)),
            dma((chips,)),
            dma((chips,)),
            dma((chips,)),
            dma((n_pb,)),
            dma((n_pb,)),
            dma((n_ga,)),
            dma((n_ga,)),
            dma((n_pb,)),
            dma((n_pb,)),
        ],
        compiler_params=pltpu.CompilerParams(
            vmem_limit_bytes=60 * 2**20, collective_id=collective_id, has_side_effects=True
        ),
        name="whole",
    )(step, offsets, offsets, query_points, cotangent, slab_ids, rel_cells, latent, w_in, b_in[None], w_out, b_out[None])


def shards(*args):
    def run(step, collective_id):
        return tuple(call(step, collective_id, *args))

    def left(state):
        return state[1][5][0, 119] > 0

    def again(state):
        step, sums = state
        new = run(step, 1)
        return step + 1, tuple(a + b for a, b in zip(sums[:5], new[:5])) + (new[5],)

    sums = run(jnp.zeros((1,), I32), 0)
    _, sums = lax.while_loop(left, again, (jnp.ones((1,), I32), sums))
    return sums[0], sums[1], sums[2][0], sums[3], sums[4][0]


def solution(mesh):
    return jax.shard_map(
        shards,
        mesh=mesh,
        in_specs=(
            P(None, "pb"),
            P(None, "pb"),
            P(None, "pb"),
            P(None, "pb"),
            P("ga", "pb"),
            P("ga", None, "pb"),
            P(),
            P(),
            P(),
            P(),
        ),
        out_specs=(P("ga", None, "pb"), P(), P(), P(), P()),
        check_vma=False,
    )
```

time: 98.3 us -> 56.6 us (0.58)
  blocking collectives: 24.8 us -> 0 us
  between operations: 14.2 us -> 0.74 us
  Pallas kernels: 42 us -> 49.1 us
  other arithmetic: 5.54 us -> 0 us
  waiting for transfers between devices: 3.75 us -> 0 us
  local copies, waits for them, and re-layouts: 7.52 us -> 5.79 us
    all_gather x2 -> x0, blocking collectives: 24.8 us -> none  [the longest x1 14 us: shards(): sums = jnp.sum(lax.all_gather(sums, 'ga', axis=0), 0)]
    pallas_call x2 -> x1, Pallas kernels: 42 us -> 49.1 us  [call(): pl.pallas_call(functools.partial(kernel, n_pb, n_ga, float(queries * n_pb...]
    concatenate x4 -> x0, local copies, waits for them, and re-layouts: 3.42 us -> none  [the longest x1 2.22 us: shards(): jnp.concatenate([cotangent, p_hi, p_lo, p_hi, ones, jnp.zeros((EXTRA - 12...]
    convert_element_type x3 -> x0, other arithmetic: 3.34 us -> none  [the longest x1 1.78 us: shards(): received.astype(F32)]
    all_gather x1 -> x0, waiting for transfers between devices: 3.05 us -> none  [shards(): slab_feats = lax.all_gather(latent[0], 'pb', axis=1, tiled=True)]
    unnamed x11 -> x26, local copies, waits for them, and re-layouts: 1.57 us -> 4.52 us
    another operation x2 -> x0, other arithmetic: 1.33 us -> none  [the longest x1 0.67 us: shards(): bo_parts = jnp.stack(split(b_out, 3), 1)]
    slice x5 -> x1, local copies, waits for them, and re-layouts: 2.09 us -> 1.26 us  [left(): return state[1][5][0, 119] > 0]
  transfers between devices with their start and end apart: 2 -> 0, of which waited for: 1 -> 0; matrix products, arithmetic and copies ran while one was open for 10% -> 0% of each run, Pallas kernels for 43% -> 0%
where the time goes in v1:
time: 56.6 us; the launch traced here: 56.3 us
  Pallas kernels  49.1 us (87%)
  local copies, waits for them, and re-layouts  5.79 us (10%)
  between operations  0.74 us (1%)
  loops' own time  0.66 us (1%)
    pallas_call x1, Pallas kernels, call(): pl.pallas_call(functools.partial(kernel, n_pb, n_ga, float(queries * n_pb...  49.1 us
    unnamed x26, local copies, waits for them, and re-layouts  4.52 us
    slice x1, local copies, waits for them, and re-layouts, left(): return state[1][5][0, 119] > 0  1.26 us

profile of v1, /device:TPU:0, one launch (start us, length us, event | category | flops | bytes accessed | tf_op | source)
XLA Modules:
  0.0 56.3 jit_solution(3404177052375428525)
XLA Ops:
  0.6 0.0 copy-start.11
  0.6 0.7 %copy-done.11 = f32[80,6]{0,1:T(8,128)S(1)} copy-done((f32[80,6]{0,1:T(8,128)S(1)}, f32[80,6]{0,1:T(8,128)}, u32[]{:S(2)}) %copy-start.11) | copy-done | bytes 1944
  1.3 0.0 copy-start.7
  1.3 0.0 copy-start.8
  1.3 0.0 copy-start.9
  1.3 0.0 copy-start.10
  1.3 0.1 copy.15.win_ref
  1.4 0.6 %copy-done.7 = bf16[64,80]{1,0:T(8,128)(2,1)S(1)} copy-done((bf16[64,80]{1,0:T(8,128)(2,1)S(1)}, bf16[64,80]{1,0:T(8,128)(2,1)}, u32[]{:S(2)}) %copy-start.7) | copy-done | bytes 10264
  2.0 0.0 copy-done.8
  2.0 0.0 copy-done.9
  2.0 0.0 copy-done.10
  2.0 0.0 copy-start
  2.1 0.0 copy-start.1
  2.1 0.0 copy-start.2
  2.1 0.0 copy-start.3
  2.1 0.0 copy-start.4
  2.1 49.1 %whole.2 = (f32[1,64,2048]{2,1,0:T(8,128)S(1)}, f32[80,6]{1,0:T(8,128)S(1)}, f32[1,80]{1,0:T(1,128)S(1)}, f32[64,80]{1,0:T(8,128)S(1)}, f32[1,64]{1,0:T(1,128)S(1)}, /*index=5*/f32[8,128]{1,0:T(8,128)}) custom-call(s32[1]{0:T(128)} %constant.8.clone.1.step_ref, s32[1,32]{1,0:T(1,128)S(1)} %copy-done.8, s32[1,32]{1,0:T(1,128)S(1)} %copy-done.8, ...), custom_call_target="tpu_custom_call" | custom-call | tf_op jit(solution)/shard_map/whole/pallas_call | solution.py:462
  51.2 0.0 copy-done
  51.2 0.0 copy-done.1
  51.2 0.0 copy-done.2
  51.2 0.0 copy-done.3
  51.2 0.0 copy-done.4
  51.2 1.9 %while.20 = (s32[1]{0:T(128)}, f32[1,64,2048]{2,1,0:T(8,128)S(1)}, f32[80,6]{1,0:T(8,128)S(1)}, f32[1,80]{1,0:T(1,128)S(1)}, f32[64,80]{1,0:T(8,128)S(1)}, /*ind...) while((s32[1]{0:T(128)}, f32[1,64,2048]{2,1,0:T(8,128)S(1)}, ...), condition=%wide.region_1.0_spmd, body=%wide.region_0.0_spmd | while | flops 136818 | bytes 1733989 | solution.py:538
  51.2 1.3 %slice.3 = f32[1,1]{1,0:T(1,128)} slice(f32[8,128]{1,0:T(8,128)} %get-tuple-element.191), slice={[0:1], [119:120]} | slice | bytes 8 | tf_op jit(solution)/shard_map/while/cond/slice | solution.py:530
  53.2 0.7 %copy.17 = f32[80,6]{0,1:T(8,128)} copy(f32[80,6]{1,0:T(8,128)S(1)} %get-tuple-element.136) | data formatting | bytes 3840
  53.8 0.8 %copy.45 = f32[1,64,2048]{2,1,0:T(8,128)} copy(f32[1,64,2048]{2,1,0:T(8,128)S(1)} %get-tuple-element.324) | data formatting | bytes 1048576
  54.6 0.5 copy.46
  55.1 0.6 %copy.47 = f32[64,80]{1,0:T(8,128)} copy(f32[64,80]{1,0:T(8,128)S(1)} %get-tuple-element.327) | data formatting | bytes 40960
  55.8 0.5 copy.48
Async XLA Ops:
  0.6 0.7 %copy-start.11 = (f32[80,6]{0,1:T(8,128)S(1)}, f32[80,6]{0,1:T(8,128)}, u32[]{:S(2)}) copy-start(f32[80,6]{0,1:T(8,128)} %param.18) | copy-start | bytes 5764
  1.3 0.7 %copy-start.7 = (bf16[64,80]{1,0:T(8,128)(2,1)S(1)}, bf16[64,80]{1,0:T(8,128)(2,1)}, u32[]{:S(2)}) copy-start(bf16[64,80]{1,0:T(8,128)(2,1)} %wout_ref.1) | copy-start | bytes 30724
  1.3 0.7 %copy-start.8 = (s32[1,32]{1,0:T(1,128)S(1)}, s32[1,32]{1,0:T(1,128)}, u32[]{:S(2)}) copy-start(s32[1,32]{1,0:T(1,128)} %offv_ref.1) | copy-start | bytes 388
  1.3 0.7 %copy-start.9 = (f32[80]{0:T(128)S(1)}, f32[80]{0:T(128)}, u32[]{:S(2)}) copy-start(f32[80]{0:T(128)} %param.19) | copy-start | bytes 964
  1.3 0.7 %copy-start.10 = (f32[64]{0:T(128)S(1)}, f32[64]{0:T(128)}, u32[]{:S(2)}) copy-start(f32[64]{0:T(128)} %param.21) | copy-start | bytes 772
  2.0 49.1 %copy-start = (bf16[64,4096]{1,0:T(8,128)(2,1)S(1)}, bf16[64,4096]{1,0:T(8,128)(2,1)}, u32[]{:S(2)}) copy-start(bf16[64,4096]{1,0:T(8,128)(2,1)} %cot_ref.1) | copy-start | bytes 1572868
  2.1 49.1 %copy-start.1 = (bf16[1,64,2048]{2,1,0:T(8,128)(2,1)S(1)}, bf16[1,64,2048]{2,1,0:T(8,128)(2,1)}, u32[]{:S(2)}) copy-start(bf16[1,64,2048]{2,1,0:T(8,128)(2,1)} %latent_ref.1) | copy-start | bytes 786436
  2.1 49.1 %copy-start.2 = (s32[8,4096]{1,0:T(8,128)S(1)}, s32[8,4096]{1,0:T(8,128)}, u32[]{:S(2)}) copy-start(s32[8,4096]{1,0:T(8,128)} %ids_ref.1) | copy-start | bytes 393220
  2.1 49.1 %copy-start.3 = (s32[8,4096]{1,0:T(8,128)S(1)}, s32[8,4096]{1,0:T(8,128)}, u32[]{:S(2)}) copy-start(s32[8,4096]{1,0:T(8,128)} %rel_ref.1) | copy-start | bytes 393220
  2.1 49.1 %copy-start.4 = (f32[3,4096]{1,0:T(4,128)S(1)}, f32[3,4096]{1,0:T(4,128)}, u32[]{:S(2)}) copy-start(f32[3,4096]{1,0:T(4,128)} %qp_ref.1) | copy-start | bytes 147460

commit v2 on v1

--- a/solution.py
+++ b/solution.py
@@ -70,10 +70,10 @@
 
 
 def weights(win_ref, bin_ref, wout_ref, bout_ref, pad_ref, w1_ref, w2_ref, w2t_ref):
-    hid, channels = win_ref.shape[0], wout_ref.shape[0]
+    hid, channels = win_ref.shape[1], wout_ref.shape[0]
     pad_ref[...] = jnp.zeros_like(pad_ref)
-    pad_ref[:hid, : win_ref.shape[1]] = win_ref[...]
-    wide = pad_ref[:hid, :]
+    pad_ref[: win_ref.shape[0], :hid] = win_ref[...]
+    wide = pad_ref[...].T[:hid]
     w_hi = wide.astype(BF16)
     w_lo = (wide - w_hi.astype(F32)).astype(BF16)
     k, col = rows_of((LANES, LANES)), cols_of((LANES, LANES))
@@ -81,6 +81,7 @@
     s_lo = mask_of(((k < 3) & (col == k + 24)) | ((k >= 3) & (k < 6) & (col == k + 29)))
     w1 = dot(w_hi, s_hi) + dot(w_lo, s_lo)
     pad_ref[0:1, :hid] = bin_ref[...]
+    pad_ref[0:1, hid:] = jnp.zeros((1, LANES - hid), F32)
     diag = jnp.where(rows_of((hid, LANES)) == cols_of((hid, LANES)), pad_ref[0:1, :], 0.0)
     for i, part in enumerate(split3(diag)):
         w1 += dot(part, mask_of(col == 3 + i))
@@ -126,22 +127,33 @@
 
 
 def kernel(
-    n_pb, n_ga, scale,
-    step_ref, offs_ref, offv_ref, qp_ref, cot_ref, ids_ref, rel_ref, latent_ref, win_ref, bin_ref, wout_ref, bout_ref,
-    grid_ref, gwin_ref, gbin_ref, gwout_ref, gbout_ref, more_ref,
+    n_pb, n_ga,
+    n_ins, latent_in, *rest,
+):
+    ins, rest = rest[:n_ins], rest[n_ins:]
+    outs, rest = rest[:3], rest[3:]
+    held, rest = rest[:n_ins], rest[n_ins:]
+    ready, rest = rest[:3], rest[3:]
+    body(n_pb, n_ga, latent_in, ins, outs, held, ready, *rest)
+
+
+def body(
+    n_pb, n_ga, latent_in, ins, outs, held, ready,
     pts_ref, pos_ref, from_ref, upto_ref, pad_ref, w1_ref, w2_ref, w2t_ref, tablev_ref, table_ref,
     cots_ref, hid_ref, slope_ref, x_ref, spot_ref, parts_ref, sums_ref, feats_ref,
     near_ref, nearin_ref, far_ref, farin_ref, own_ref, acc_ref,
     ar_ref, arin_ref, gaall_ref, fin_ref,
-    table_sem, gsend, grecv, fsend, nsend, nrecv, rsend, rrecv, asend, arecv, bsend, brecv, csend, crecv,
+    in_sem, latent_sem, out_sem, table_sem, gsend, grecv, fsend, nsend, nrecv, rsend, rrecv, asend, arecv, bsend, brecv, csend, crecv,
 ):
+    offs_ref, offv_ref, win_ref, bin_ref, wout_ref, bout_ref, ids_ref, qp_ref, rel_ref, cot_ref = held[:10]
+    gridv_ref, final_ref, more_ref = ready
     me, slab = lax.axis_index("pb"), lax.axis_index("ga")
     chips = n_pb // 2
     chip, core = me // 2, me % 2
     sibling = chip * 2 + 1 - core
     tiles = cot_ref.shape[1] // TILE
-    channels, hid = cot_ref.shape[0], win_ref.shape[0]
-    blocks = latent_ref.shape[2] // LANES
+    channels, hid = cot_ref.shape[0], win_ref.shape[1]
+    blocks = latent_in.shape[2] // LANES
     limit = blocks * n_pb - SPAN
     group = math.gcd(tiles, 4)
 
@@ -157,30 +169,38 @@
         return lax.rem(chip + chips - m, chips) * 2 + core
 
     barrier = pltpu.get_barrier_semaphore()
+    mine = me * blocks
+    latent_copies = [
+        pltpu.make_async_copy(latent_in.at[0, :, pl.ds(b * LANES, LANES)], feats_ref.at[mine + b], latent_sem.at[b])
+        for b in range(blocks)
+    ]
+    loads = [pltpu.make_async_copy(src, dst, in_sem.at[i]) for i, (src, dst) in enumerate(zip(ins, held))]
+    for copy in latent_copies + loads:
+        copy.start()
     for m in range(1, n_pb):
         pl.semaphore_signal(barrier, inc=1, device_id={"pb": lax.rem(me + m, n_pb)}, device_id_type=MESH)
     for m in range(1, n_ga):
         pl.semaphore_signal(barrier, inc=1, device_id={"ga": lax.rem(slab + m, n_ga)}, device_id_type=MESH)
 
-    mine = me * blocks
-    for b in range(blocks):
-        feats_ref[mine + b] = latent_ref[0, :, b * LANES : (b + 1) * LANES]
-    pts_ref[...] = jnp.ones_like(pts_ref)
-    pts_ref[0:3, :] = qp_ref[...]
-    order_parts(tiles, limit, offv_ref, tablev_ref)
-    weights(win_ref, bin_ref, wout_ref, bout_ref, pad_ref, w1_ref, w2_ref, w2t_ref)
-
-    pl.semaphore_wait(barrier, n_pb - 1 + n_ga - 1)
-
     def feats_of(d):
         return feats_ref.at[pl.ds(d * blocks, blocks)]
 
+    for copy in latent_copies:
+        copy.wait()
+    pl.semaphore_wait(barrier, n_pb - 1 + n_ga - 1)
     out = []
     for m in range(1, chips):
         out.append(send(feats_of(me), feats_of(me), gsend.at[m], grecv.at[me], {"pb": peer(m)}))
     out.append(send(feats_of(me), feats_of(me), gsend.at[0], grecv.at[me], {"pb": sibling}))
     for copy in out:
         copy.start()
+
+    for copy in loads:
+        copy.wait()
+    pts_ref[...] = jnp.ones_like(pts_ref)
+    pts_ref[0:3, :] = qp_ref[...]
+    order_parts(tiles, limit, offv_ref, tablev_ref)
+    weights(win_ref, bin_ref, wout_ref, bout_ref, pad_ref, w1_ref, w2_ref, w2t_ref)
     table_copy = pltpu.make_async_copy(tablev_ref, table_ref, table_sem)
     table_copy.start()
 
@@ -192,7 +212,7 @@
     total = dot(packed, jnp.ones((TILE, TILE), BF16))
     r, c = rows_of((rows, rows)), cols_of((rows, rows))
     start = dot(mask_of((r // KN == c // KN) & (c < r)), total.astype(BF16))
-    skip = (step_ref[0] * CAP).astype(F32)
+    skip = (held[10][0] * CAP).astype(F32) if len(held) > 10 else 0.0
     pos_ref[...] = jnp.where(live > 0, before + start - skip, -1.0e6)
     from_ref[...] = start - skip
     upto_ref[...] = start + total - skip
@@ -202,7 +222,7 @@
     def tile_base(t):
         return jnp.minimum(lax.shift_right_logical(offs_ref[0, t], 7), limit)
 
-    def query_side(t):
+    def draw(t):
         cols = pl.ds(pl.multiple_of(t * TILE, TILE), TILE)
         lines = pl.ds(pl.multiple_of(t * KN, KN), KN)
         base = tile_base(t)
@@ -219,8 +239,11 @@
         p_hi = points.astype(BF16).astype(F32)
         small = jnp.concatenate([p_hi, points - p_hi, low, high], 0).astype(BF16)
         data = jnp.concatenate([cot_ref[:, cols], small], 0)
-        drawn = dot_nt(data, pick)
-        cot = drawn[:channels]
+        return dot_nt(data, pick)
+
+    def place_inputs(t, drawn):
+        lines = pl.ds(pl.multiple_of(t * KN, KN), KN)
+        base = tile_base(t)
         head = drawn[channels : channels + 16]
         wide_from = jnp.concatenate([from_ref[lines, :]] * (CAP // TILE), 1)
         wide_upto = jnp.concatenate([upto_ref[lines, :]] * (CAP // TILE), 1)
@@ -243,12 +266,7 @@
         )
         centre = jnp.where(row < 3, (along.astype(F32) + 0.5) / GX, 0.0)
         x = jnp.concatenate([head, centre, head[:8], centre, jnp.zeros((8, CAP), F32)], 0).astype(BF16)
-        hidden, slope = gelu_parts(dot(w1_ref[:, :XR], x))
-        hidden = hidden.astype(BF16)
-        kern = dot(w2_ref[...], jnp.concatenate([hidden, x], 0))
-        grad = (kern * cot).astype(BF16)
-        part = dot_nt(spread(hi, grad), lane_onehot(lo))
-        return cot.astype(BF16), hidden, slope, x, jnp.where(row < 4, lo, hi), part
+        return x, lo, hi
 
     def lane_onehot(lo):
         row = jnp.broadcast_to(lo[:1], (LANES, CAP)).astype(BF16)
@@ -265,13 +283,26 @@
         return jnp.concatenate(pieces, 0)
 
     def first(i, carry):
-        done = [(i * group + u, query_side(i * group + u)) for u in range(group)]
-        for t, (cot, hidden, slope, x, spot, part) in done:
-            cots_ref[t] = cot
+        ts = [i * group + u for u in range(group)]
+        drawn = [draw(t) for t in ts]
+        placed = [place_inputs(t, d) for t, d in zip(ts, drawn)]
+        cots = [d[:channels].astype(BF16) for d in drawn]
+        pres = [dot(w1_ref[:, :XR], x) for x, _, _ in placed]
+        kerns = []
+        for t, pre, cot, (x, lo, hi) in zip(ts, pres, cots, placed):
+            hidden, slope = gelu_parts(pre)
+            hidden = hidden.astype(BF16)
+            kerns.append(dot(w2_ref[...], jnp.concatenate([hidden, x], 0)))
             hid_ref[t] = hidden
             slope_ref[t] = slope
+            cots_ref[t] = cot
             x_ref[t] = x
-            spot_ref[t] = spot
+            spot_ref[t] = jnp.where(rows_of((8, CAP)) < 4, lo, hi)
+        parts = []
+        for kern, cot, (x, lo, hi) in zip(kerns, cots, placed):
+            grad = (kern * cot.astype(F32)).astype(BF16)
+            parts.append(dot_nt(spread(hi, grad), lane_onehot(lo)))
+        for t, part in zip(ts, parts):
             for j in range(SPAN):
                 parts_ref[j * tiles + t] = part[j * channels : (j + 1) * channels]
         return carry
@@ -348,21 +379,27 @@
 
     acc_ref[...] = jnp.zeros_like(acc_ref)
 
-    def feature_side(t):
-        spot = spot_ref[t]
-        hi = jnp.broadcast_to(spot[4:5], (8, CAP))
+    def draw_feats(t):
         window = feats_ref[pl.ds(tile_base(t), SPAN)].reshape(SPAN * channels, LANES)
-        drawn = dot(window, lane_onehot(spot))
-        tall = jnp.concatenate([hi] * (channels // 8), 0)
+        return dot(window, lane_onehot(spot_ref[t]))
+
+    def feats_grad(t, drawn):
+        tall = jnp.broadcast_to(spot_ref[t][4:5], (channels, CAP))
         feats = drawn[:channels]
         for j in range(1, SPAN):
             feats = jnp.where(tall == float(j), drawn[j * channels : (j + 1) * channels], feats)
-        grad_kernel = (feats * cots_ref[t].astype(F32)).astype(BF16)
-        grad_pre = (dot(w2t_ref[...], grad_kernel) * slope_ref[t]).astype(BF16)
-        return dot_nt(jnp.concatenate([grad_kernel, grad_pre], 0), jnp.concatenate([hid_ref[t], x_ref[t]], 0))
+        return (feats * cots_ref[t].astype(F32)).astype(BF16)
 
     def second(i, carry):
-        acc_ref[...] += functools.reduce(lambda a, b: a + b, [feature_side(i * group + u) for u in range(group)])
+        ts = [i * group + u for u in range(group)]
+        drawn = [draw_feats(t) for t in ts]
+        grads = [feats_grad(t, d) for t, d in zip(ts, drawn)]
+        pres = [dot(w2t_ref[...], g) for g in grads]
+        sums = []
+        for t, g, p in zip(ts, grads, pres):
+            both = jnp.concatenate([g, (p * slope_ref[t]).astype(BF16)], 0)
+            sums.append(dot_nt(both, jnp.concatenate([hid_ref[t], x_ref[t]], 0)))
+        acc_ref[...] += functools.reduce(lambda a, b: a + b, sums)
         return carry
 
     lax.fori_loop(0, tiles // group, second, 0)
@@ -418,25 +455,21 @@
         value = own_ref[b]
         for m in range(1, chips):
             value += farin_ref[m - 1, b].astype(F32)
-        grid_ref[0, :, b * LANES : (b + 1) * LANES] = value
+        gridv_ref[0, :, b * LANES : (b + 1) * LANES] = value
+    stores = [pltpu.make_async_copy(src, dst, out_sem.at[i]) for i, (src, dst) in enumerate(zip(ready, outs))]
+    stores[0].start()
 
     for m in range(1, n_pb):
         d = lax.rem(me + m, n_pb)
         send(fin_ref.at[d], fin_ref.at[d], csend.at[m - 1], crecv.at[d], {"pb": d}).wait_recv()
     final = fin_ref[...].reshape(channels, LANES)
-    gwout_ref[...] = final[:, :hid] * scale
-    more_ref[...] = jnp.broadcast_to(final[0:1, :], more_ref.shape)
-
-    def chosen(shift):
-        return jnp.where(((l < 3) & (k == shift + l)) | ((l >= 3) & (l < 6) & (k == shift + 1 + l)) | ((l == 6) & (k == shift + 3)), scale, 0.0)
-
-    taken = jnp.concatenate([exact(final, chosen(112)), exact(final[:tail], chosen(120))], 0)
-    gwin_ref[...] = taken[:, : gwin_ref.shape[1]]
-    pick6 = jnp.where(cols_of((8, LANES)) == 6, 1.0, 0.0)
-    gbin_ref[...] = exact_nt(pick6, taken)[0:1]
-    pickb = jnp.where(cols_of((8, LANES)) == hid + 3, scale, 0.0)
-    gbout_ref[...] = exact_nt(pickb, final)[0:1]
-
+    final_ref[...] = final
+    flags = jnp.where(cols_of((1, LANES)) == 119, final[0:1], 0.0)
+    more_ref[0] = jnp.sum(flags).astype(I32)
+    for copy in stores[1:]:
+        copy.start()
+    for copy in stores:
+        copy.wait()
     for copy in out + forwards + first_hop + second_hop + third_hop:
         copy.wait_send()
     for m in range(chips):
@@ -455,23 +488,24 @@
     blocks = owned // LANES
     pairs = SPAN * tiles
     lanes = -(-pairs // LANES) * LANES
-    vmem = pl.BlockSpec(memory_space=pltpu.VMEM)
-    smem = pl.BlockSpec(memory_space=pltpu.SMEM)
+    hbm = pl.BlockSpec(memory_space=pltpu.HBM)
     dma = pltpu.SemaphoreType.DMA
     slices = channels // n_pb
+    ins = (offsets, offsets, w_in.T, b_in[None], w_out, b_out[None], slab_ids, query_points, rel_cells, cotangent)
+    ins += () if step is None else (step,)
+    outs = [
+        ((1, channels, owned), F32),
+        ((channels, LANES), F32),
+        ((1,), I32),
+    ]
     return pl.pallas_call(
-        functools.partial(kernel, n_pb, n_ga, float(queries * n_pb) ** (-0.5)),
-        out_shape=[
-            jax.ShapeDtypeStruct((1, channels, owned), F32),
-            jax.ShapeDtypeStruct(w_in.shape, F32),
-            jax.ShapeDtypeStruct((1, hid), F32),
-            jax.ShapeDtypeStruct(w_out.shape, F32),
-            jax.ShapeDtypeStruct((1, channels), F32),
-            jax.ShapeDtypeStruct((8, LANES), F32),
-        ],
-        in_specs=[smem, smem] + [vmem] * 10,
-        out_specs=[vmem] * 6,
-        scratch_shapes=[
+        functools.partial(kernel, n_pb, n_ga, len(ins)),
+        out_shape=[jax.ShapeDtypeStruct(*o) for o in outs],
+        in_specs=[hbm] * (1 + len(ins)),
+        out_specs=[hbm] * len(outs),
+        scratch_shapes=[(pltpu.SMEM if i in (0, 10) else pltpu.VMEM)(a.shape, a.dtype) for i, a in enumerate(ins)]
+        + [pltpu.VMEM(*outs[0]), pltpu.VMEM(*outs[1]), pltpu.SMEM(*outs[2])]
+        + [
             pltpu.VMEM((8, queries), F32),
             pltpu.VMEM((tiles * KN, TILE), F32),
             pltpu.VMEM((tiles * KN, TILE), F32),
@@ -500,6 +534,9 @@
             pltpu.VMEM((n_pb, slices, LANES), F32),
             pltpu.VMEM((n_ga, slices, LANES), F32),
             pltpu.VMEM((n_pb, slices, LANES), F32),
+            dma((len(ins),)),
+            dma((blocks,)),
+            dma((len(outs),)),
             dma,
             dma((chips,)),
             dma((n_pb,)),
@@ -516,27 +553,77 @@
             dma((n_pb,)),
         ],
         compiler_params=pltpu.CompilerParams(
-            vmem_limit_bytes=60 * 2**20, collective_id=collective_id, has_side_effects=True
+            vmem_limit_bytes=67043328, collective_id=collective_id, has_side_effects=True
         ),
         name="whole",
-    )(step, offsets, offsets, query_points, cotangent, slab_ids, rel_cells, latent, w_in, b_in[None], w_out, b_out[None])
+    )(latent, *ins)
+
+
+def settle(scale, grid_in, final_in, grid_ref, *rest):
+    smalls, (final_ref, hold_ref), ready = rest[:4], rest[4:6], rest[6:10]
+    load_sem, in_sem, out_sem, small_sem = rest[10:]
+    gwin_ref, gbin_ref, gwout_ref, gbout_ref = ready
+    load = pltpu.make_async_copy(final_in, final_ref, load_sem)
+    load.start()
+    parts = out_sem.shape[0]
+    wide = grid_ref.shape[2] // parts
+    arrive, leave = [], []
+    for i in range(parts):
+        at = (0, slice(None), pl.ds(i * wide, wide))
+        arrive.append(pltpu.make_async_copy(grid_in.at[at], hold_ref.at[at], in_sem.at[i]))
+        leave.append(pltpu.make_async_copy(hold_ref.at[at], grid_ref.at[at], out_sem.at[i]))
+        arrive[-1].start()
+    load.wait()
+    channels, hid = gwout_ref.shape
+    final = final_ref[...]
+    k, l = rows_of((LANES, LANES)), cols_of((LANES, LANES))
+
+    def chosen(shift):
+        along = (l < 3) & (k == shift + l)
+        cells = (l >= 3) & (l < 6) & (k == shift + 1 + l)
+        return jnp.where(along | cells | ((l == 6) & (k == shift + 3)), scale, 0.0)
+
+    gwout_ref[...] = final[:, :hid] * scale
+    taken = jnp.concatenate([exact(final, chosen(112)), exact(final[: hid - channels], chosen(120))], 0)
+    turned = exact_nt(jnp.where(rows_of((8, LANES)) == cols_of((8, LANES)), 1.0, 0.0), taken)
+    gwin_ref[...] = turned[: gwin_ref.shape[0]]
+    gbin_ref[...] = turned[6:7]
+    gbout_ref[...] = exact_nt(jnp.where(cols_of((8, LANES)) == hid + 3, scale, 0.0), final)[0:1]
+    for i in range(parts):
+        arrive[i].wait()
+        leave[i].start()
+    stores = [pltpu.make_async_copy(src, dst, small_sem.at[i]) for i, (src, dst) in enumerate(zip(ready, smalls))]
+    for copy in stores:
+        copy.start()
+    for copy in leave + stores:
+        copy.wait()
 
 
 def shards(*args):
-    def run(step, collective_id):
-        return tuple(call(step, collective_id, *args))
-
-    def left(state):
-        return state[1][5][0, 119] > 0
-
     def again(state):
-        step, sums = state
-        new = run(step, 1)
-        return step + 1, tuple(a + b for a, b in zip(sums[:5], new[:5])) + (new[5],)
-
-    sums = run(jnp.zeros((1,), I32), 0)
-    _, sums = lax.while_loop(left, again, (jnp.ones((1,), I32), sums))
-    return sums[0], sums[1], sums[2][0], sums[3], sums[4][0]
+        step, _, sums = state
+        grid, final, more = call(step, 1, *args)
+        return step + 1, more, (sums[0] + grid, sums[1] + final)
+
+    grid, final, more = call(None, 0, *args)
+    first = (jnp.ones((1,), I32), more, (grid, final))
+    grid, final = lax.while_loop(lambda state: state[1][0] > 0, again, first)[2]
+    hid, channels = args[6].shape[0], args[8].shape[0]
+    queries = args[0].shape[1] * lax.axis_size("pb")
+    hbm = pl.BlockSpec(memory_space=pltpu.HBM)
+    dma = pltpu.SemaphoreType.DMA
+    parts = math.gcd(grid.shape[2] // LANES, 4)
+    shapes = [args[6].shape[::-1], (1, hid), (channels, hid), (1, channels)]
+    grid, gwin, gbin, gwout, gbout = pl.pallas_call(
+        functools.partial(settle, float(queries) ** (-0.5)),
+        out_shape=[jax.ShapeDtypeStruct(v, F32) for v in [grid.shape] + shapes],
+        in_specs=[hbm] * 2,
+        out_specs=[hbm] * 5,
+        scratch_shapes=[pltpu.VMEM(v, F32) for v in [final.shape, grid.shape] + shapes]
+        + [dma, dma((parts,)), dma((parts,)), dma((4,))],
+        name="settle",
+    )(grid, final)
+    return grid, gwin.T, gbin[0], gwout, gbout[0]
 
 
 def solution(mesh):

time: 56.6 us -> 44.6 us (0.79)
  Pallas kernels: 49.1 us -> 43.2 us
  local copies, waits for them, and re-layouts: 5.79 us -> 0 us
    pallas_call x1 -> x2, Pallas kernels: 49.1 us -> 43.2 us  [the longest x1 40.8 us: call(): pl.pallas_call(functools.partial(kernel, n_pb, n_ga, len(ins)), out_shape...]
    unnamed x26 -> x0, local copies, waits for them, and re-layouts: 4.52 us -> none
    slice x1 -> x0, local copies, waits for them, and re-layouts: 1.26 us -> none  [left(): return state[1][5][0, 119] > 0]
where the time goes in v2:
time: 44.6 us; the launch traced here: 44.5 us
  Pallas kernels  43.2 us (97%)
  between operations  0.65 us (1%)
  loops' own time  0.64 us (1%)
    pallas_call x1, Pallas kernels, call(): pl.pallas_call(functools.partial(kernel, n_pb, n_ga, len(ins)), out_shape...  40.8 us
    pallas_call x1, Pallas kernels, shards(): pl.pallas_call(functools.partial(settle, float(queries) ** (-0.5)), out_s...  2.34 us

profile of v2, /device:TPU:0, one launch (start us, length us, event | category | flops | bytes accessed | tf_op | source)
XLA Modules:
  0.0 44.5 jit_solution(15483272523036962299)
XLA Ops:
  0.6 40.8 %whole.2 = (f32[1,64,2048]{2,1,0:T(8,128)}, f32[64,128]{1,0:T(8,128)}, s32[1]{0:T(128)}) custom-call(bf16[1,64,2048]{2,1,0:T(8,128)(2,1)} %latent_in.1, s32[1,32]{1,0:T(1,128)} %rest_1_.1, s32[1,32]{1,0:T(1,128)} %rest_1_.1, f32[6,80]{1,0:T(8,128)} %bitcast.14, f32[1,80]{1,0:T(1,128)} %bitcast.16, bf16[64,80]{1,0:T(8,128)(2,1)} %rest_4_.1, ...), custom_call_target="tpu_custom_call" | custom-call | tf_op jit(solution)/shard_map/whole/pallas_call | solution.py:501
  41.5 0.6 %while.14 = (s32[1]{0:T(128)}, s32[1]{0:T(128)}, f32[1,64,2048]{2,1,0:T(8,128)}, f32[64,128]{1,0:T(8,128)}, f32[80,6]{0,1:T(8,128)}, /*index=5*/f32[80]{0:T(128)...) while((s32[1]{0:T(128)}, s32[1]{0:T(128)}, ...), condition=%wide.region_1.0_spmd, body=%wide.region_0.0_spmd | while | flops 139266 | bytes 2064617 | solution.py:610
  42.1 2.3 %settle.1 = (f32[1,64,2048]{2,1,0:T(8,128)}, f32[6,80]{1,0:T(8,128)}, f32[1,80]{1,0:T(1,128)}, f32[64,80]{1,0:T(8,128)}, f32[1,64]{1,0:T(1,128)}) custom-call(f32[1,64,2048]{2,1,0:T(8,128)} %get-tuple-element.91.grid_in, f32[64,128]{1,0:T(8,128)} %get-tuple-element.92.final_in), custom_call_target="tpu_custom_call" | custom-call | tf_op jit(solution)/shard_map/settle/pallas_call | solution.py:617

commit v3 on v2

--- a/solution.py
+++ b/solution.py
@@ -141,9 +141,9 @@
     n_pb, n_ga, latent_in, ins, outs, held, ready,
     pts_ref, pos_ref, from_ref, upto_ref, pad_ref, w1_ref, w2_ref, w2t_ref, tablev_ref, table_ref,
     cots_ref, hid_ref, slope_ref, x_ref, spot_ref, parts_ref, sums_ref, feats_ref,
-    near_ref, nearin_ref, far_ref, farin_ref, own_ref, acc_ref,
+    near_ref, nearin_ref, far_ref, farin_ref, half_ref, own_ref, acc_ref,
     ar_ref, arin_ref, gaall_ref, fin_ref,
-    in_sem, latent_sem, out_sem, table_sem, gsend, grecv, fsend, nsend, nrecv, rsend, rrecv, asend, arecv, bsend, brecv, csend, crecv,
+    in_sem, latent_sem, out_sem, table_sem, gsend, grecv, fsend, nsend, nrecv, rsend, rrecv, hsend, hrecv, asend, arecv, bsend, brecv, csend, crecv,
 ):
     offs_ref, offv_ref, win_ref, bin_ref, wout_ref, bout_ref, ids_ref, qp_ref, rel_ref, cot_ref = held[:10]
     gridv_ref, final_ref, more_ref = ready
@@ -162,11 +162,17 @@
             src_ref=src, dst_ref=dst, send_sem=ssem, recv_sem=rsem, device_id=where, device_id_type=MESH
         )
 
-    def peer(m):
-        return lax.rem(chip + m, chips) * 2 + core
-
-    def peer_back(m):
-        return lax.rem(chip + chips - m, chips) * 2 + core
+    square = chips == 4 and blocks % 2 == 0
+    if square:
+        beside = chip + 1 - 2 * (chip % 2)
+        above = lax.rem(chip + 2, 4)
+        others = [beside, above, lax.rem(beside + 2, 4)]
+    else:
+        others = [lax.rem(chip + m, chips) for m in range(1, chips)]
+    peers = [o * 2 + core for o in others]
+    twins = [o * 2 + 1 - core for o in others]
+    near_chips = others + [chip]
+    half = blocks // 2
 
     barrier = pltpu.get_barrier_semaphore()
     mine = me * blocks
@@ -188,10 +194,21 @@
     for copy in latent_copies:
         copy.wait()
     pl.semaphore_wait(barrier, n_pb - 1 + n_ga - 1)
+    def half_of(d, h):
+        return feats_ref.at[pl.ds(d * blocks + h * half, half)]
+
+    def piece(d, h, ssem, to):
+        return send(half_of(d, h), half_of(d, h), ssem, grecv.at[d, h], {"pb": to})
+
     out = []
-    for m in range(1, chips):
-        out.append(send(feats_of(me), feats_of(me), gsend.at[m], grecv.at[me], {"pb": peer(m)}))
-    out.append(send(feats_of(me), feats_of(me), gsend.at[0], grecv.at[me], {"pb": sibling}))
+    if square:
+        for i in range(2):
+            out.append(piece(me, 1 - i, gsend.at[1 + i], peers[0]))
+            out.append(piece(me, i, gsend.at[3 + i], peers[1]))
+    else:
+        for i, to in enumerate(peers):
+            out.append(send(feats_of(me), feats_of(me), gsend.at[1 + i], grecv.at[me, 0], {"pb": to}))
+    out.append(send(feats_of(me), feats_of(me), gsend.at[0], grecv.at[me, 0], {"pb": sibling}))
     for copy in out:
         copy.start()
 
@@ -307,7 +324,18 @@
                 parts_ref[j * tiles + t] = part[j * channels : (j + 1) * channels]
         return carry
 
-    lax.fori_loop(0, tiles // group, first, 0)
+    steps = tiles // group
+    middle = steps // 2
+    lax.fori_loop(0, middle, first, 0)
+    forwards = []
+    if square:
+        piece(peers[0], 1, gsend.at[0], peers[0]).wait_recv()
+        forwards.append(piece(peers[0], 1, hsend.at[2], peers[1]))
+        piece(peers[1], 0, gsend.at[0], peers[1]).wait_recv()
+        forwards.append(piece(peers[1], 0, hsend.at[3], peers[0]))
+        for copy in forwards:
+            copy.start()
+    lax.fori_loop(middle, steps, first, 0)
 
     table_copy.wait()
 
@@ -326,56 +354,83 @@
     def block(b):
         return sums_ref[pair_at(2, b)] * table_ref[3, b].astype(F32)
 
-    def near_copy(m):
-        return send(near_ref.at[m], nearin_ref.at[m], nsend.at[m], nrecv.at[m], {"pb": sibling})
-
-    pair = math.gcd(blocks, 4)
-    order = [m % chips for m in range(1, chips + 1)]
-    for i, m in enumerate(order):
-        owner = lax.rem(chip + m, chips) * 2 + 1 - core
-
-        def fill(b, carry, m=m, owner=owner):
-            for u in range(pair):
-                near_ref[m, b * pair + u] = block(owner * blocks + b * pair + u).astype(BF16)
-            return carry
-
-        lax.fori_loop(0, blocks // pair, fill, 0)
-        if i > 0:
-            near_copy(order[i - 1]).start()
-    forwards = []
-    for m in range(1, chips):
-        d = peer_back(m)
-        send(feats_of(d), feats_of(d), gsend.at[m], grecv.at[d], {"pb": d}).wait_recv()
-        copy = send(feats_of(d), feats_of(d), fsend.at[m - 1], grecv.at[d], {"pb": sibling})
+    def near_copy(i):
+        return send(near_ref.at[i], nearin_ref.at[i], nsend.at[i], nrecv.at[i], {"pb": sibling})
+
+    def pass_on(i):
+        d = peers[i]
+        copy = send(feats_of(d), feats_of(d), fsend.at[i], grecv.at[d, 0], {"pb": sibling})
         copy.start()
         forwards.append(copy)
-        if m == 1:
-            near_copy(order[-1]).start()
-
-    def far_copy(m):
-        return send(far_ref.at[m - 1], farin_ref.at[m - 1], rsend.at[m - 1], rrecv.at[m - 1], {"pb": peer(m)})
-
-    for i, m in enumerate(order):
-        owner = lax.rem(chip + m, chips) * 2 + core
-        near_copy(m).wait_recv()
-
-        def join(b, carry, m=m, owner=owner):
+
+    pair = math.gcd(blocks, 4)
+    order = list(range(chips - 2, -1, -1)) + [chips - 1]
+    if square:
+        piece(peers[0], 0, gsend.at[0], peers[0]).wait_recv()
+        pass_on(0)
+        piece(peers[1], 1, gsend.at[0], peers[1]).wait_recv()
+        pass_on(1)
+    for n, i in enumerate(order):
+        owner = near_chips[i] * 2 + 1 - core
+
+        def fill(b, carry, i=i, owner=owner):
+            for u in range(pair):
+                near_ref[i, b * pair + u] = block(owner * blocks + b * pair + u).astype(BF16)
+            return carry
+
+        lax.fori_loop(0, blocks // pair, fill, 0)
+        if n > 0:
+            near_copy(order[n - 1]).start()
+    if square:
+        piece(peers[2], 0, gsend.at[0], peers[2]).wait_recv()
+        near_copy(order[-1]).start()
+        piece(peers[2], 1, gsend.at[0], peers[2]).wait_recv()
+        pass_on(2)
+    else:
+        for i, d in enumerate(peers):
+            send(feats_of(d), feats_of(d), gsend.at[0], grecv.at[d, 0], {"pb": d}).wait_recv()
+            pass_on(i)
+        near_copy(order[-1]).start()
+
+    if square:
+        early = [(2, 0, 0, half_ref.at[0], 0), (2, 1, 1, half_ref.at[1], 1)]
+        early += [(0, 0, 0, farin_ref.at[0, pl.ds(0, half)], 2), (1, 1, 1, farin_ref.at[1, pl.ds(half, half)], 5)]
+        late = [(0, 1, 0, farin_ref.at[0, pl.ds(half, half)], 3), (1, 0, 1, farin_ref.at[1, pl.ds(0, half)], 4)]
+
+        def far_half(slot, h, to, dst, n):
+            return send(far_ref.at[slot, pl.ds(h * half, half)], dst, hsend.at[4 + n], hrecv.at[n], {"pb": peers[to]})
+
+        early = [far_half(*e) for e in early]
+        late = [far_half(*e) for e in late]
+        slots = [(early[0], early[1]), (early[2],), (early[3],)]
+    else:
+        fars = [
+            send(far_ref.at[i], farin_ref.at[i], rsend.at[i], rrecv.at[i], {"pb": to}) for i, to in enumerate(peers)
+        ]
+        slots = [(fars[i],) for i in order[:-1]]
+    if square:
+        order = [2, 0, 1, 3]
+    for n, i in enumerate(order):
+        owner = near_chips[i] * 2 + core
+        near_copy(i).wait_recv()
+
+        def join(b, carry, i=i, owner=owner):
             for u in range(pair):
                 at = b * pair + u
-                value = block(owner * blocks + at) + nearin_ref[m, at].astype(F32)
-                if m:
-                    far_ref[m - 1, at] = value.astype(BF16)
+                value = block(owner * blocks + at) + nearin_ref[i, at].astype(F32)
+                if i < chips - 1:
+                    far_ref[i, at] = value.astype(BF16)
                 else:
                     own_ref[at] = value
             return carry
 
         lax.fori_loop(0, blocks // pair, join, 0)
-        if i > 0:
-            far_copy(order[i - 1]).start()
-
-    for m in range(chips):
-        d = lax.rem(chip + m, chips) * 2 + 1 - core
-        send(feats_of(d), feats_of(d), gsend.at[0], grecv.at[d], {"pb": sibling}).wait_recv()
+        if n > 0:
+            for copy in slots[n - 1]:
+                copy.start()
+
+    for d in twins + [sibling]:
+        send(feats_of(d), feats_of(d), gsend.at[0], grecv.at[d, 0], {"pb": sibling}).wait_recv()
 
     acc_ref[...] = jnp.zeros_like(acc_ref)
 
@@ -428,10 +483,18 @@
         copy = send(ar_ref.at[to], arin_ref.at[me], asend.at[m - 1], arecv.at[me], {"pb": to})
         copy.start()
         first_hop.append(copy)
+    if square:
+        for i, copy in enumerate(early[:2]):
+            copy.wait_recv()
+            into = far_ref.at[1 - i, pl.ds(i * half, half)]
+            into[...] = (into[...].astype(F32) + half_ref[i].astype(F32)).astype(BF16)
     for m in range(1, n_pb):
         d = lax.rem(me + m, n_pb)
         send(ar_ref.at[d], arin_ref.at[d], asend.at[m - 1], arecv.at[d], {"pb": d}).wait_recv()
     gaall_ref[pl.ds(slab, 1)] = jnp.sum(arin_ref[...], 0, keepdims=True)
+    if square:
+        for copy in late:
+            copy.start()
     second_hop = []
     for m in range(1, n_ga):
         to = lax.rem(slab + m, n_ga)
@@ -449,12 +512,12 @@
         copy.start()
         third_hop.append(copy)
 
-    for m in range(1, chips):
-        far_copy(m).wait_recv()
+    for copy in early[2:] + late if square else fars:
+        copy.wait_recv()
     for b in range(blocks):
         value = own_ref[b]
-        for m in range(1, chips):
-            value += farin_ref[m - 1, b].astype(F32)
+        for i in range(2 if square else chips - 1):
+            value += farin_ref[i, b].astype(F32)
         gridv_ref[0, :, b * LANES : (b + 1) * LANES] = value
     stores = [pltpu.make_async_copy(src, dst, out_sem.at[i]) for i, (src, dst) in enumerate(zip(ready, outs))]
     stores[0].start()
@@ -472,10 +535,10 @@
         copy.wait()
     for copy in out + forwards + first_hop + second_hop + third_hop:
         copy.wait_send()
-    for m in range(chips):
-        near_copy(m).wait_send()
-    for m in range(1, chips):
-        far_copy(m).wait_send()
+    for i in range(chips):
+        near_copy(i).wait_send()
+    for copy in early + late if square else fars:
+        copy.wait_send()
 
 
 def call(step, collective_id, query_points, cotangent, slab_ids, rel_cells, offsets, latent, w_in, b_in, w_out, b_out):
@@ -528,6 +591,7 @@
             pltpu.VMEM((chips, blocks, channels, LANES), BF16),
             pltpu.VMEM((chips - 1, blocks, channels, LANES), BF16),
             pltpu.VMEM((chips - 1, blocks, channels, LANES), BF16),
+            pltpu.VMEM((2, max(blocks // 2, 1), channels, LANES), BF16),
             pltpu.VMEM((blocks, channels, LANES), F32),
             pltpu.VMEM((channels + hid, LANES), F32),
             pltpu.VMEM((n_pb, slices, LANES), F32),
@@ -538,13 +602,15 @@
             dma((blocks,)),
             dma((len(outs),)),
             dma,
-            dma((chips,)),
-            dma((n_pb,)),
+            dma((max(chips + 1, 5),)),
+            dma((n_pb, 2)),
             dma((chips,)),
             dma((chips,)),
             dma((chips,)),
             dma((chips,)),
             dma((chips,)),
+            dma((10,)),
+            dma((6,)),
             dma((n_pb,)),
             dma((n_pb,)),
             dma((n_ga,)),

time: 44.6 us -> 39.9 us (0.89)
  Pallas kernels: 43.2 us -> 38.5 us
    pallas_call x1, Pallas kernels: 40.8 us -> 36.1 us  [call(): pl.pallas_call(functools.partial(kernel, n_pb, n_ga, len(ins)), out_shape...]
where the time goes in v3:
time: 39.9 us; the launch traced here: 39.8 us
  Pallas kernels  38.5 us (96%)
  between operations  0.65 us (2%)
  loops' own time  0.64 us (2%)
    pallas_call x1, Pallas kernels, call(): pl.pallas_call(functools.partial(kernel, n_pb, n_ga, len(ins)), out_shape...  36.1 us
    pallas_call x1, Pallas kernels, shards(): pl.pallas_call(functools.partial(settle, float(queries) ** (-0.5)), out_s...  2.34 us

profile of v3, /device:TPU:0, one launch (start us, length us, event | category | flops | bytes accessed | tf_op | source)
XLA Modules:
  0.0 39.8 jit_solution(8448343637648593318)
XLA Ops:
  0.6 36.1 %whole.2 = (f32[1,64,2048]{2,1,0:T(8,128)}, f32[64,128]{1,0:T(8,128)}, s32[1]{0:T(128)}) custom-call(bf16[1,64,2048]{2,1,0:T(8,128)(2,1)} %latent_in.1, s32[1,32]{1,0:T(1,128)} %rest_1_.1, s32[1,32]{1,0:T(1,128)} %rest_1_.1, f32[6,80]{1,0:T(8,128)} %bitcast.14, f32[1,80]{1,0:T(1,128)} %bitcast.16, bf16[64,80]{1,0:T(8,128)(2,1)} %rest_4_.1, ...), custom_call_target="tpu_custom_call" | custom-call | tf_op jit(solution)/shard_map/whole/pallas_call | solution.py:564
  36.8 0.6 %while.14 = (s32[1]{0:T(128)}, s32[1]{0:T(128)}, f32[1,64,2048]{2,1,0:T(8,128)}, f32[64,128]{1,0:T(8,128)}, f32[80,6]{0,1:T(8,128)}, /*index=5*/f32[80]{0:T(128)...) while((s32[1]{0:T(128)}, s32[1]{0:T(128)}, ...), condition=%wide.region_1.0_spmd, body=%wide.region_0.0_spmd | while | flops 139266 | bytes 2064617 | solution.py:676
  37.4 2.3 %settle.1 = (f32[1,64,2048]{2,1,0:T(8,128)}, f32[6,80]{1,0:T(8,128)}, f32[1,80]{1,0:T(1,128)}, f32[64,80]{1,0:T(8,128)}, f32[1,64]{1,0:T(1,128)}) custom-call(f32[1,64,2048]{2,1,0:T(8,128)} %get-tuple-element.91.grid_in, f32[64,128]{1,0:T(8,128)} %get-tuple-element.92.final_in), custom_call_target="tpu_custom_call" | custom-call | tf_op jit(solution)/shard_map/settle/pallas_call | solution.py:683

commit v4 on v3

--- a/solution.py
+++ b/solution.py
@@ -133,20 +133,19 @@
     ins, rest = rest[:n_ins], rest[n_ins:]
     outs, rest = rest[:3], rest[3:]
     held, rest = rest[:n_ins], rest[n_ins:]
-    ready, rest = rest[:3], rest[3:]
-    body(n_pb, n_ga, latent_in, ins, outs, held, ready, *rest)
+    body(n_pb, n_ga, latent_in, ins, outs, held, *rest)
 
 
 def body(
-    n_pb, n_ga, latent_in, ins, outs, held, ready,
+    n_pb, n_ga, latent_in, ins, outs, held, more_ref,
     pts_ref, pos_ref, from_ref, upto_ref, pad_ref, w1_ref, w2_ref, w2t_ref, tablev_ref, table_ref,
     cots_ref, hid_ref, slope_ref, x_ref, spot_ref, parts_ref, sums_ref, feats_ref,
     near_ref, nearin_ref, far_ref, farin_ref, half_ref, own_ref, acc_ref,
     ar_ref, arin_ref, gaall_ref, fin_ref,
-    in_sem, latent_sem, out_sem, table_sem, gsend, grecv, fsend, nsend, nrecv, rsend, rrecv, hsend, hrecv, asend, arecv, bsend, brecv, csend, crecv,
+    in_sem, latent_sem, out_sem, table_sem, gsend, grecv, fsend, frecv, nsend, nrecv, rsend, rrecv, hsend, hrecv, asend, arecv, bsend, brecv, csend, crecv,
 ):
     offs_ref, offv_ref, win_ref, bin_ref, wout_ref, bout_ref, ids_ref, qp_ref, rel_ref, cot_ref = held[:10]
-    gridv_ref, final_ref, more_ref = ready
+    grid_ref, final_ref, more_out = outs
     me, slab = lax.axis_index("pb"), lax.axis_index("ga")
     chips = n_pb // 2
     chip, core = me // 2, me % 2
@@ -170,14 +169,13 @@
     else:
         others = [lax.rem(chip + m, chips) for m in range(1, chips)]
     peers = [o * 2 + core for o in others]
-    twins = [o * 2 + 1 - core for o in others]
     near_chips = others + [chip]
     half = blocks // 2
 
     barrier = pltpu.get_barrier_semaphore()
     mine = me * blocks
     latent_copies = [
-        pltpu.make_async_copy(latent_in.at[0, :, pl.ds(b * LANES, LANES)], feats_ref.at[mine + b], latent_sem.at[b])
+        pltpu.make_async_copy(latent_in.at[0, :, pl.ds(b * LANES, LANES)], feats_ref.at[mine + b], latent_sem)
         for b in range(blocks)
     ]
     loads = [pltpu.make_async_copy(src, dst, in_sem.at[i]) for i, (src, dst) in enumerate(zip(ins, held))]
@@ -191,24 +189,23 @@
     def feats_of(d):
         return feats_ref.at[pl.ds(d * blocks, blocks)]
 
-    for copy in latent_copies:
-        copy.wait()
+    pltpu.make_async_copy(feats_of(me), feats_of(me), latent_sem).wait()
     pl.semaphore_wait(barrier, n_pb - 1 + n_ga - 1)
     def half_of(d, h):
         return feats_ref.at[pl.ds(d * blocks + h * half, half)]
 
-    def piece(d, h, ssem, to):
-        return send(half_of(d, h), half_of(d, h), ssem, grecv.at[d, h], {"pb": to})
+    def piece(slot, d, h, ssem, to):
+        return send(half_of(d, h), half_of(d, h), ssem, grecv.at[slot, h], {"pb": to})
 
     out = []
     if square:
         for i in range(2):
-            out.append(piece(me, 1 - i, gsend.at[1 + i], peers[0]))
-            out.append(piece(me, i, gsend.at[3 + i], peers[1]))
+            out.append(piece(0, me, 1 - i, gsend, peers[0]))
+            out.append(piece(1, me, i, gsend, peers[1]))
     else:
         for i, to in enumerate(peers):
-            out.append(send(feats_of(me), feats_of(me), gsend.at[1 + i], grecv.at[me, 0], {"pb": to}))
-    out.append(send(feats_of(me), feats_of(me), gsend.at[0], grecv.at[me, 0], {"pb": sibling}))
+            out.append(send(feats_of(me), feats_of(me), gsend, grecv.at[i, 0], {"pb": to}))
+    out.append(send(feats_of(me), feats_of(me), gsend, frecv, {"pb": sibling}))
     for copy in out:
         copy.start()
 
@@ -325,18 +322,33 @@
         return carry
 
     steps = tiles // group
-    middle = steps // 2
+
+    def pass_half(i, h):
+        return send(half_of(peers[i], h), half_of(peers[i], h), fsend, frecv, {"pb": sibling})
+
+    def come(i, h):
+        piece(i, peers[i], h, gsend, peers[i]).wait_recv()
+
+    middle, late_step, ahead = steps // 2, steps * 7 // 8, steps // 4
     lax.fori_loop(0, middle, first, 0)
-    forwards = []
-    if square:
-        piece(peers[0], 1, gsend.at[0], peers[0]).wait_recv()
-        forwards.append(piece(peers[0], 1, hsend.at[2], peers[1]))
-        piece(peers[1], 0, gsend.at[0], peers[1]).wait_recv()
-        forwards.append(piece(peers[1], 0, hsend.at[3], peers[0]))
-        for copy in forwards:
-            copy.start()
-    lax.fori_loop(middle, steps, first, 0)
-
+    if square:
+        come(0, 1)
+        piece(2, peers[0], 1, hsend, peers[1]).start()
+        come(1, 0)
+        piece(2, peers[1], 0, hsend, peers[0]).start()
+        pass_half(0, 1).start()
+        pass_half(1, 0).start()
+    lax.fori_loop(middle, late_step, first, 0)
+    if square:
+        for i in range(2):
+            come(i, i)
+            pass_half(i, i).start()
+    lax.fori_loop(late_step, steps, first, 0)
+
+    if square:
+        for h in range(2):
+            come(2, h)
+            pass_half(2, h).start()
     table_copy.wait()
 
     def pair_at(line, b):
@@ -355,21 +367,10 @@
         return sums_ref[pair_at(2, b)] * table_ref[3, b].astype(F32)
 
     def near_copy(i):
-        return send(near_ref.at[i], nearin_ref.at[i], nsend.at[i], nrecv.at[i], {"pb": sibling})
-
-    def pass_on(i):
-        d = peers[i]
-        copy = send(feats_of(d), feats_of(d), fsend.at[i], grecv.at[d, 0], {"pb": sibling})
-        copy.start()
-        forwards.append(copy)
+        return send(near_ref.at[i], nearin_ref.at[i], nsend, nrecv.at[i], {"pb": sibling})
 
     pair = math.gcd(blocks, 4)
     order = list(range(chips - 2, -1, -1)) + [chips - 1]
-    if square:
-        piece(peers[0], 0, gsend.at[0], peers[0]).wait_recv()
-        pass_on(0)
-        piece(peers[1], 1, gsend.at[0], peers[1]).wait_recv()
-        pass_on(1)
     for n, i in enumerate(order):
         owner = near_chips[i] * 2 + 1 - core
 
@@ -381,56 +382,14 @@
         lax.fori_loop(0, blocks // pair, fill, 0)
         if n > 0:
             near_copy(order[n - 1]).start()
-    if square:
-        piece(peers[2], 0, gsend.at[0], peers[2]).wait_recv()
-        near_copy(order[-1]).start()
-        piece(peers[2], 1, gsend.at[0], peers[2]).wait_recv()
-        pass_on(2)
-    else:
-        for i, d in enumerate(peers):
-            send(feats_of(d), feats_of(d), gsend.at[0], grecv.at[d, 0], {"pb": d}).wait_recv()
-            pass_on(i)
-        near_copy(order[-1]).start()
-
-    if square:
-        early = [(2, 0, 0, half_ref.at[0], 0), (2, 1, 1, half_ref.at[1], 1)]
-        early += [(0, 0, 0, farin_ref.at[0, pl.ds(0, half)], 2), (1, 1, 1, farin_ref.at[1, pl.ds(half, half)], 5)]
-        late = [(0, 1, 0, farin_ref.at[0, pl.ds(half, half)], 3), (1, 0, 1, farin_ref.at[1, pl.ds(0, half)], 4)]
-
-        def far_half(slot, h, to, dst, n):
-            return send(far_ref.at[slot, pl.ds(h * half, half)], dst, hsend.at[4 + n], hrecv.at[n], {"pb": peers[to]})
-
-        early = [far_half(*e) for e in early]
-        late = [far_half(*e) for e in late]
-        slots = [(early[0], early[1]), (early[2],), (early[3],)]
-    else:
-        fars = [
-            send(far_ref.at[i], farin_ref.at[i], rsend.at[i], rrecv.at[i], {"pb": to}) for i, to in enumerate(peers)
-        ]
-        slots = [(fars[i],) for i in order[:-1]]
-    if square:
-        order = [2, 0, 1, 3]
-    for n, i in enumerate(order):
-        owner = near_chips[i] * 2 + core
-        near_copy(i).wait_recv()
-
-        def join(b, carry, i=i, owner=owner):
-            for u in range(pair):
-                at = b * pair + u
-                value = block(owner * blocks + at) + nearin_ref[i, at].astype(F32)
-                if i < chips - 1:
-                    far_ref[i, at] = value.astype(BF16)
-                else:
-                    own_ref[at] = value
-            return carry
-
-        lax.fori_loop(0, blocks // pair, join, 0)
-        if n > 0:
-            for copy in slots[n - 1]:
-                copy.start()
-
-    for d in twins + [sibling]:
-        send(feats_of(d), feats_of(d), gsend.at[0], grecv.at[d, 0], {"pb": sibling}).wait_recv()
+    if not square:
+        for i in range(chips - 1):
+            d = lax.rem(chip + chips - 1 - i, chips) * 2 + core
+            send(feats_of(d), feats_of(d), gsend, grecv.at[i, 0], {"pb": d}).wait_recv()
+            send(feats_of(d), feats_of(d), fsend, frecv, {"pb": sibling}).start()
+
+    all_twins = feats_ref.at[pl.ds(0, chips * blocks)]
+    send(all_twins, all_twins, gsend, frecv, {"pb": sibling}).wait_recv()
 
     acc_ref[...] = jnp.zeros_like(acc_ref)
 
@@ -457,7 +416,46 @@
         acc_ref[...] += functools.reduce(lambda a, b: a + b, sums)
         return carry
 
-    lax.fori_loop(0, tiles // group, second, 0)
+    near_copy(order[-1]).start()
+    lax.fori_loop(0, ahead, second, 0)
+    if square:
+        early = [(2, 0, 0, half_ref.at[0], 0), (2, 1, 1, half_ref.at[1], 1)]
+        early += [(0, 0, 0, farin_ref.at[0, pl.ds(0, half)], 2), (1, 1, 1, farin_ref.at[1, pl.ds(half, half)], 2)]
+        late = [(0, 1, 0, farin_ref.at[0, pl.ds(half, half)], 2), (1, 0, 1, farin_ref.at[1, pl.ds(0, half)], 2)]
+
+        def far_half(slot, h, to, dst, n):
+            return send(far_ref.at[slot, pl.ds(h * half, half)], dst, hsend, hrecv.at[n], {"pb": peers[to]})
+
+        early = [far_half(*e) for e in early]
+        late = [far_half(*e) for e in late]
+        slots = [(early[0], early[1]), (early[2],), (early[3],)]
+    else:
+        fars = [
+            send(far_ref.at[i], farin_ref.at[i], rsend.at[i], rrecv.at[i], {"pb": to}) for i, to in enumerate(peers)
+        ]
+        slots = [(fars[i],) for i in order[:-1]]
+    if square:
+        order = [2, 0, 1, 3]
+    for n, i in enumerate(order):
+        owner = near_chips[i] * 2 + core
+        near_copy(i).wait_recv()
+
+        def join(b, carry, i=i, owner=owner):
+            for u in range(pair):
+                at = b * pair + u
+                value = block(owner * blocks + at) + nearin_ref[i, at].astype(F32)
+                if i < chips - 1:
+                    far_ref[i, at] = value.astype(BF16)
+                else:
+                    own_ref[at] = value
+            return carry
+
+        lax.fori_loop(0, blocks // pair, join, 0)
+        if n > 0:
+            for copy in slots[n - 1]:
+                copy.start()
+
+    lax.fori_loop(ahead, steps, second, 0)
 
     k, l = rows_of((LANES, LANES)), cols_of((LANES, LANES))
 
@@ -471,73 +469,70 @@
     top += exact(acc_ref[channels : 2 * channels], gathered(112))
     rest = exact(acc_ref[2 * channels : 2 * channels + tail], gathered(120))
     flag = jnp.where(left > 0, 1.0, 0.0)
-    corner = (rows_of((tail, LANES)) == 0) & (cols_of((tail, LANES)) == 119)
-    rest = jnp.where(corner, flag, rest)
+    slices = channels // n_pb
     top = jnp.concatenate([top[:tail] + rest, top[tail:]], 0)
-    slices = channels // n_pb
+    marked = (lax.rem(rows_of((channels, LANES)), slices) == 0) & (cols_of((channels, LANES)) == LANES - 1)
+    top = jnp.where(marked, flag, top)
     ar_ref[...] = top.reshape(n_pb, slices, LANES)
     arin_ref[pl.ds(me, 1)] = ar_ref[pl.ds(me, 1)]
-    first_hop = []
     for m in range(1, n_pb):
         to = lax.rem(me + m, n_pb)
-        copy = send(ar_ref.at[to], arin_ref.at[me], asend.at[m - 1], arecv.at[me], {"pb": to})
-        copy.start()
-        first_hop.append(copy)
+        send(ar_ref.at[to], arin_ref.at[me], asend, arecv, {"pb": to}).start()
     if square:
         for i, copy in enumerate(early[:2]):
             copy.wait_recv()
             into = far_ref.at[1 - i, pl.ds(i * half, half)]
             into[...] = (into[...].astype(F32) + half_ref[i].astype(F32)).astype(BF16)
-    for m in range(1, n_pb):
-        d = lax.rem(me + m, n_pb)
-        send(ar_ref.at[d], arin_ref.at[d], asend.at[m - 1], arecv.at[d], {"pb": d}).wait_recv()
+    most = pl.ds(0, n_pb - 1)
+    all_in = send(ar_ref.at[most], arin_ref.at[most], asend, arecv, {"pb": sibling})
+    all_in.wait_recv()
     gaall_ref[pl.ds(slab, 1)] = jnp.sum(arin_ref[...], 0, keepdims=True)
+    for m in range(1, n_ga):
+        to = lax.rem(slab + m, n_ga)
+        send(gaall_ref.at[slab], gaall_ref.at[slab], bsend, brecv, {"ga": to}).start()
     if square:
         for copy in late:
             copy.start()
-    second_hop = []
-    for m in range(1, n_ga):
-        to = lax.rem(slab + m, n_ga)
-        copy = send(gaall_ref.at[slab], gaall_ref.at[slab], bsend.at[m - 1], brecv.at[slab], {"ga": to})
-        copy.start()
-        second_hop.append(copy)
-    for m in range(1, n_ga):
-        d = lax.rem(slab + m, n_ga)
-        send(gaall_ref.at[d], gaall_ref.at[d], bsend.at[m - 1], brecv.at[d], {"ga": d}).wait_recv()
-    fin_ref[pl.ds(me, 1)] = jnp.sum(gaall_ref[...], 0, keepdims=True)
-    third_hop = []
+    less = gaall_ref.at[pl.ds(0, n_ga - 1)]
+    all_slabs = send(less, less, bsend, brecv, {"pb": sibling})
+    all_slabs.wait_recv()
+    settled = jnp.sum(gaall_ref[...], 0, keepdims=True)
+    fin_ref[pl.ds(me, 1)] = settled
+    more_ref[0] = jnp.sum(jnp.where(cols_of((1, LANES)) == LANES - 1, settled[0, 0:1], 0.0)).astype(I32)
     for m in range(1, n_pb):
         to = lax.rem(me + m, n_pb)
-        copy = send(fin_ref.at[me], fin_ref.at[me], csend.at[m - 1], crecv.at[me], {"pb": to})
-        copy.start()
-        third_hop.append(copy)
-
-    for copy in early[2:] + late if square else fars:
-        copy.wait_recv()
+        send(fin_ref.at[me], fin_ref.at[me], csend, crecv, {"pb": to}).start()
+    tell = pltpu.make_async_copy(more_ref, more_out, out_sem)
+    tell.start()
+
+    if square:
+        come_in = farin_ref.at[pl.ds(0, 2)]
+        send(come_in, come_in, hsend, hrecv.at[2], {"pb": sibling}).wait_recv()
+    else:
+        for copy in fars:
+            copy.wait_recv()
     for b in range(blocks):
         value = own_ref[b]
         for i in range(2 if square else chips - 1):
             value += farin_ref[i, b].astype(F32)
-        gridv_ref[0, :, b * LANES : (b + 1) * LANES] = value
-    stores = [pltpu.make_async_copy(src, dst, out_sem.at[i]) for i, (src, dst) in enumerate(zip(ready, outs))]
-    stores[0].start()
-
-    for m in range(1, n_pb):
-        d = lax.rem(me + m, n_pb)
-        send(fin_ref.at[d], fin_ref.at[d], csend.at[m - 1], crecv.at[d], {"pb": d}).wait_recv()
+        grid_ref[0, :, b * LANES : (b + 1) * LANES] = value
+
+    all_final = send(fin_ref.at[most], fin_ref.at[most], csend, crecv, {"pb": sibling})
+    all_final.wait_recv()
     final = fin_ref[...].reshape(channels, LANES)
     final_ref[...] = final
-    flags = jnp.where(cols_of((1, LANES)) == 119, final[0:1], 0.0)
-    more_ref[0] = jnp.sum(flags).astype(I32)
-    for copy in stores[1:]:
-        copy.start()
-    for copy in stores:
-        copy.wait()
-    for copy in out + forwards + first_hop + second_hop + third_hop:
-        copy.wait_send()
-    for i in range(chips):
-        near_copy(i).wait_send()
-    for copy in early + late if square else fars:
+    tell.wait()
+    all_feats = feats_ref.at[pl.ds(0, (3 if square else chips) * blocks)]
+    send(all_feats, all_feats, gsend, frecv, {"pb": sibling}).wait_send()
+    passed = feats_ref.at[pl.ds(0, (chips - 1) * blocks)]
+    send(passed, passed, fsend, frecv, {"pb": sibling}).wait_send()
+    send(near_ref, nearin_ref, nsend, nrecv.at[0], {"pb": sibling}).wait_send()
+    if square:
+        send(all_twins, all_twins, hsend, frecv, {"pb": sibling}).wait_send()
+    else:
+        for copy in fars:
+            copy.wait_send()
+    for copy in (all_in, all_slabs, all_final):
         copy.wait_send()
 
 
@@ -552,6 +547,7 @@
     pairs = SPAN * tiles
     lanes = -(-pairs // LANES) * LANES
     hbm = pl.BlockSpec(memory_space=pltpu.HBM)
+    vmem = pl.BlockSpec(memory_space=pltpu.VMEM)
     dma = pltpu.SemaphoreType.DMA
     slices = channels // n_pb
     ins = (offsets, offsets, w_in.T, b_in[None], w_out, b_out[None], slab_ids, query_points, rel_cells, cotangent)
@@ -565,9 +561,9 @@
         functools.partial(kernel, n_pb, n_ga, len(ins)),
         out_shape=[jax.ShapeDtypeStruct(*o) for o in outs],
         in_specs=[hbm] * (1 + len(ins)),
-        out_specs=[hbm] * len(outs),
+        out_specs=[vmem, vmem, hbm],
         scratch_shapes=[(pltpu.SMEM if i in (0, 10) else pltpu.VMEM)(a.shape, a.dtype) for i, a in enumerate(ins)]
-        + [pltpu.VMEM(*outs[0]), pltpu.VMEM(*outs[1]), pltpu.SMEM(*outs[2])]
+        + [pltpu.SMEM(*outs[2])]
         + [
             pltpu.VMEM((8, queries), F32),
             pltpu.VMEM((tiles * KN, TILE), F32),
@@ -599,47 +595,39 @@
             pltpu.VMEM((n_ga, slices, LANES), F32),
             pltpu.VMEM((n_pb, slices, LANES), F32),
             dma((len(ins),)),
-            dma((blocks,)),
-            dma((len(outs),)),
-            dma,
-            dma((max(chips + 1, 5),)),
-            dma((n_pb, 2)),
+            dma,
+            dma,
+            dma,
+            dma,
+            dma((chips - 1, 2)),
+            dma,
+            dma,
+            dma,
             dma((chips,)),
             dma((chips,)),
             dma((chips,)),
-            dma((chips,)),
-            dma((chips,)),
-            dma((10,)),
-            dma((6,)),
-            dma((n_pb,)),
-            dma((n_pb,)),
-            dma((n_ga,)),
-            dma((n_ga,)),
-            dma((n_pb,)),
-            dma((n_pb,)),
+            dma,
+            dma((3,)),
+            dma,
+            dma,
+            dma,
+            dma,
+            dma,
+            dma,
         ],
         compiler_params=pltpu.CompilerParams(
-            vmem_limit_bytes=67043328, collective_id=collective_id, has_side_effects=True
+            vmem_limit_bytes=67043328 - 4 * channels * (owned + LANES) - 1024, collective_id=collective_id, has_side_effects=True
         ),
         name="whole",
     )(latent, *ins)
 
 
-def settle(scale, grid_in, final_in, grid_ref, *rest):
-    smalls, (final_ref, hold_ref), ready = rest[:4], rest[4:6], rest[6:10]
-    load_sem, in_sem, out_sem, small_sem = rest[10:]
+def settle(scale, grid_in, final_ref, grid_ref, *rest):
+    smalls, ready = rest[:4], rest[4:8]
+    grid_sem, small_sem = rest[8:]
     gwin_ref, gbin_ref, gwout_ref, gbout_ref = ready
-    load = pltpu.make_async_copy(final_in, final_ref, load_sem)
-    load.start()
-    parts = out_sem.shape[0]
-    wide = grid_ref.shape[2] // parts
-    arrive, leave = [], []
-    for i in range(parts):
-        at = (0, slice(None), pl.ds(i * wide, wide))
-        arrive.append(pltpu.make_async_copy(grid_in.at[at], hold_ref.at[at], in_sem.at[i]))
-        leave.append(pltpu.make_async_copy(hold_ref.at[at], grid_ref.at[at], out_sem.at[i]))
-        arrive[-1].start()
-    load.wait()
+    move = pltpu.make_async_copy(grid_in, grid_ref, grid_sem)
+    move.start()
     channels, hid = gwout_ref.shape
     final = final_ref[...]
     k, l = rows_of((LANES, LANES)), cols_of((LANES, LANES))
@@ -655,14 +643,12 @@
     gwin_ref[...] = turned[: gwin_ref.shape[0]]
     gbin_ref[...] = turned[6:7]
     gbout_ref[...] = exact_nt(jnp.where(cols_of((8, LANES)) == hid + 3, scale, 0.0), final)[0:1]
-    for i in range(parts):
-        arrive[i].wait()
-        leave[i].start()
     stores = [pltpu.make_async_copy(src, dst, small_sem.at[i]) for i, (src, dst) in enumerate(zip(ready, smalls))]
     for copy in stores:
         copy.start()
-    for copy in leave + stores:
+    for copy in stores:
         copy.wait()
+    move.wait()
 
 
 def shards(*args):
@@ -678,15 +664,13 @@
     queries = args[0].shape[1] * lax.axis_size("pb")
     hbm = pl.BlockSpec(memory_space=pltpu.HBM)
     dma = pltpu.SemaphoreType.DMA
-    parts = math.gcd(grid.shape[2] // LANES, 4)
     shapes = [args[6].shape[::-1], (1, hid), (channels, hid), (1, channels)]
     grid, gwin, gbin, gwout, gbout = pl.pallas_call(
         functools.partial(settle, float(queries) ** (-0.5)),
         out_shape=[jax.ShapeDtypeStruct(v, F32) for v in [grid.shape] + shapes],
-        in_specs=[hbm] * 2,
+        in_specs=[hbm, pl.BlockSpec(memory_space=pltpu.VMEM)],
         out_specs=[hbm] * 5,
-        scratch_shapes=[pltpu.VMEM(v, F32) for v in [final.shape, grid.shape] + shapes]
-        + [dma, dma((parts,)), dma((parts,)), dma((4,))],
+        scratch_shapes=[pltpu.VMEM(v, F32) for v in shapes] + [dma, dma((4,))],
         name="settle",
     )(grid, final)
     return grid, gwin.T, gbin[0], gwout, gbout[0]

time: 39.9 us -> 37.2 us (0.932)
  Pallas kernels: 38.5 us -> 35.8 us
    pallas_call x1, Pallas kernels: 36.1 us -> 34.7 us  [call(): pl.pallas_call(functools.partial(kernel, n_pb, n_ga, len(ins)), out_shape...]
    pallas_call x1, Pallas kernels: 2.34 us -> 1.13 us  [shards(): pl.pallas_call(functools.partial(settle, float(queries) ** (-0.5)), out_s...]
where the time goes in v4:
time: 37.2 us; the launch traced here: 37.1 us
  Pallas kernels  35.8 us (96%)
  between operations  0.65 us (2%)
  loops' own time  0.57 us (2%)
    pallas_call x1, Pallas kernels, call(): pl.pallas_call(functools.partial(kernel, n_pb, n_ga, len(ins)), out_shape...  34.7 us
    pallas_call x1, Pallas kernels, shards(): pl.pallas_call(functools.partial(settle, float(queries) ** (-0.5)), out_s...  1.13 us

profile of v4, /device:TPU:0, one launch (start us, length us, event | category | flops | bytes accessed | tf_op | source)
XLA Modules:
  0.0 37.1 jit_solution(16911215267568024972)
XLA Ops:
  0.6 34.7 %whole.2 = (f32[1,64,2048]{2,1,0:T(8,128)S(1)}, f32[64,128]{1,0:T(8,128)S(1)}, s32[1]{0:T(128)}) custom-call(bf16[1,64,2048]{2,1,0:T(8,128)(2,1)} %latent_in.1, s32[1,32]{1,0:T(1,128)} %rest_1_.1, s32[1,32]{1,0:T(1,128)} %rest_1_.1, f32[6,80]{1,0:T(8,128)} %bitcast.14, f32[1,80]{1,0:T(1,128)} %bitcast.16, bf16[64,80]{1,0:T(8,128)(2,1)} %rest_4_.1, ...), custom_call_target="tpu_custom_call" | custom-call | tf_op jit(solution)/shard_map/whole/pallas_call | solution.py:560
  35.3 0.6 %while.14 = (s32[1]{0:T(128)}, s32[1]{0:T(128)}, f32[1,64,2048]{2,1,0:T(8,128)S(1)}, f32[64,128]{1,0:T(8,128)S(1)}, f32[80,6]{0,1:T(8,128)}, /*index=5*/f32[80]{...) while((s32[1]{0:T(128)}, s32[1]{0:T(128)}, ...), condition=%wide.region_1.0_spmd, body=%wide.region_0.0_spmd | while | flops 139266 | bytes 1802417 | solution.py:662
  35.9 1.1 %settle.1 = (f32[1,64,2048]{2,1,0:T(8,128)}, f32[6,80]{1,0:T(8,128)}, f32[1,80]{1,0:T(1,128)}, f32[64,80]{1,0:T(8,128)}, f32[1,64]{1,0:T(1,128)}) custom-call(f32[1,64,2048]{2,1,0:T(8,128)S(1)} %get-tuple-element.91.grid_in, f32[64,128]{1,0:T(8,128)S(1)} %get-tuple-element.92.final_ref), custom_call_target="tpu_custom_call" | custom-call | tf_op jit(solution)/shard_map/settle/pallas_call | solution.py:668

commit v5 on v4

--- a/solution.py
+++ b/solution.py
@@ -173,6 +173,10 @@
     half = blocks // 2
 
     barrier = pltpu.get_barrier_semaphore()
+    for m in range(1, n_pb):
+        pl.semaphore_signal(barrier, inc=1, device_id={"pb": lax.rem(me + m, n_pb)}, device_id_type=MESH)
+    for m in range(1, n_ga):
+        pl.semaphore_signal(barrier, inc=1, device_id={"ga": lax.rem(slab + m, n_ga)}, device_id_type=MESH)
     mine = me * blocks
     latent_copies = [
         pltpu.make_async_copy(latent_in.at[0, :, pl.ds(b * LANES, LANES)], feats_ref.at[mine + b], latent_sem)
@@ -181,11 +185,6 @@
     loads = [pltpu.make_async_copy(src, dst, in_sem.at[i]) for i, (src, dst) in enumerate(zip(ins, held))]
     for copy in latent_copies + loads:
         copy.start()
-    for m in range(1, n_pb):
-        pl.semaphore_signal(barrier, inc=1, device_id={"pb": lax.rem(me + m, n_pb)}, device_id_type=MESH)
-    for m in range(1, n_ga):
-        pl.semaphore_signal(barrier, inc=1, device_id={"ga": lax.rem(slab + m, n_ga)}, device_id_type=MESH)
-
     def feats_of(d):
         return feats_ref.at[pl.ds(d * blocks, blocks)]
 
@@ -329,7 +328,7 @@
     def come(i, h):
         piece(i, peers[i], h, gsend, peers[i]).wait_recv()
 
-    middle, late_step, ahead = steps // 2, steps * 7 // 8, steps // 4
+    middle, late_step = steps // 2, steps * 7 // 8
     lax.fori_loop(0, middle, first, 0)
     if square:
         come(0, 1)
@@ -404,8 +403,10 @@
             feats = jnp.where(tall == float(j), drawn[j * channels : (j + 1) * channels], feats)
         return (feats * cots_ref[t].astype(F32)).astype(BF16)
 
+    wide = math.gcd(tiles, 8)
+
     def second(i, carry):
-        ts = [i * group + u for u in range(group)]
+        ts = [i * wide + u for u in range(wide)]
         drawn = [draw_feats(t) for t in ts]
         grads = [feats_grad(t, d) for t, d in zip(ts, drawn)]
         pres = [dot(w2t_ref[...], g) for g in grads]
@@ -417,6 +418,7 @@
         return carry
 
     near_copy(order[-1]).start()
+    ahead = tiles // wide // 2
     lax.fori_loop(0, ahead, second, 0)
     if square:
         early = [(2, 0, 0, half_ref.at[0], 0), (2, 1, 1, half_ref.at[1], 1)]
@@ -428,7 +430,7 @@
 
         early = [far_half(*e) for e in early]
         late = [far_half(*e) for e in late]
-        slots = [(early[0], early[1]), (early[2],), (early[3],)]
+        slots = [early[:2], [], []]
     else:
         fars = [
             send(far_ref.at[i], farin_ref.at[i], rsend.at[i], rrecv.at[i], {"pb": to}) for i, to in enumerate(peers)
@@ -455,7 +457,7 @@
             for copy in slots[n - 1]:
                 copy.start()
 
-    lax.fori_loop(ahead, steps, second, 0)
+    lax.fori_loop(ahead, tiles // wide, second, 0)
 
     k, l = rows_of((LANES, LANES)), cols_of((LANES, LANES))
 
@@ -479,6 +481,8 @@
         to = lax.rem(me + m, n_pb)
         send(ar_ref.at[to], arin_ref.at[me], asend, arecv, {"pb": to}).start()
     if square:
+        for copy in early[2:]:
+            copy.start()
         for i, copy in enumerate(early[:2]):
             copy.wait_recv()
             into = far_ref.at[1 - i, pl.ds(i * half, half)]

time: 37.2 us -> 34.8 us (0.935)
  Pallas kernels: 35.8 us -> 33.4 us
    pallas_call x1, Pallas kernels: 34.7 us -> 32.3 us  [call(): pl.pallas_call(functools.partial(kernel, n_pb, n_ga, len(ins)), out_shape...]
where the time goes in v5:
time: 34.8 us; the launch traced here: 34.6 us
  Pallas kernels  33.4 us (96%)
  between operations  0.65 us (2%)
  loops' own time  0.57 us (2%)
    pallas_call x1, Pallas kernels, call(): pl.pallas_call(functools.partial(kernel, n_pb, n_ga, len(ins)), out_shape...  32.3 us
    pallas_call x1, Pallas kernels, shards(): pl.pallas_call(functools.partial(settle, float(queries) ** (-0.5)), out_s...  1.14 us

profile of v5, /device:TPU:0, one launch (start us, length us, event | category | flops | bytes accessed | tf_op | source)
XLA Modules:
  0.0 34.6 jit_solution(5747998759442033715)
XLA Ops:
  0.6 32.3 %whole.2 = (f32[1,64,2048]{2,1,0:T(8,128)S(1)}, f32[64,128]{1,0:T(8,128)S(1)}, s32[1]{0:T(128)}) custom-call(bf16[1,64,2048]{2,1,0:T(8,128)(2,1)} %latent_in.1, s32[1,32]{1,0:T(1,128)} %rest_1_.1, s32[1,32]{1,0:T(1,128)} %rest_1_.1, f32[6,80]{1,0:T(8,128)} %bitcast.14, f32[1,80]{1,0:T(1,128)} %bitcast.16, bf16[64,80]{1,0:T(8,128)(2,1)} %rest_4_.1, ...), custom_call_target="tpu_custom_call" | custom-call | tf_op jit(solution)/shard_map/whole/pallas_call | solution.py:564
  32.9 0.6 %while.14 = (s32[1]{0:T(128)}, s32[1]{0:T(128)}, f32[1,64,2048]{2,1,0:T(8,128)S(1)}, f32[64,128]{1,0:T(8,128)S(1)}, f32[80,6]{0,1:T(8,128)}, /*index=5*/f32[80]{...) while((s32[1]{0:T(128)}, s32[1]{0:T(128)}, ...), condition=%wide.region_1.0_spmd, body=%wide.region_0.0_spmd | while | flops 139266 | bytes 1802417 | solution.py:666
  33.5 1.1 %settle.1 = (f32[1,64,2048]{2,1,0:T(8,128)}, f32[6,80]{1,0:T(8,128)}, f32[1,80]{1,0:T(1,128)}, f32[64,80]{1,0:T(8,128)}, f32[1,64]{1,0:T(1,128)}) custom-call(f32[1,64,2048]{2,1,0:T(8,128)S(1)} %get-tuple-element.91.grid_in, f32[64,128]{1,0:T(8,128)S(1)} %get-tuple-element.92.final_ref), custom_call_target="tpu_custom_call" | custom-call | tf_op jit(solution)/shard_map/settle/pallas_call | solution.py:672

commit v6 on v5

--- a/solution.py
+++ b/solution.py
@@ -141,8 +141,8 @@
     pts_ref, pos_ref, from_ref, upto_ref, pad_ref, w1_ref, w2_ref, w2t_ref, tablev_ref, table_ref,
     cots_ref, hid_ref, slope_ref, x_ref, spot_ref, parts_ref, sums_ref, feats_ref,
     near_ref, nearin_ref, far_ref, farin_ref, half_ref, own_ref, acc_ref,
-    ar_ref, arin_ref, gaall_ref, fin_ref,
-    in_sem, latent_sem, out_sem, table_sem, gsend, grecv, fsend, frecv, nsend, nrecv, rsend, rrecv, hsend, hrecv, asend, arecv, bsend, brecv, csend, crecv,
+    ar_ref, arin_ref, gaall_ref, fin_ref, marks_ref, markz_ref,
+    in_sem, latent_sem, out_sem, table_sem, gsend, grecv, fsend, frecv, nsend, nrecv, rsend, rrecv, hsend, hrecv, asend, arecv, bsend, brecv, csend, crecv, msend, mrecv, zsend, zrecv,
 ):
     offs_ref, offv_ref, win_ref, bin_ref, wout_ref, bout_ref, ids_ref, qp_ref, rel_ref, cot_ref = held[:10]
     grid_ref, final_ref, more_out = outs
@@ -231,6 +231,7 @@
     upto_ref[...] = start + total - skip
     left = jnp.max(start + total - skip - float(CAP), axis=0, keepdims=True)
     left = jnp.max(left, axis=1, keepdims=True)
+    marks_ref[pl.ds(me, 1)] = jnp.broadcast_to(jnp.where(left > 0, 1.0, 0.0)[None], (1, 8, LANES))
 
     def tile_base(t):
         return jnp.minimum(lax.shift_right_logical(offs_ref[0, t], 7), limit)
@@ -329,7 +330,11 @@
         piece(i, peers[i], h, gsend, peers[i]).wait_recv()
 
     middle, late_step = steps // 2, steps * 7 // 8
-    lax.fori_loop(0, middle, first, 0)
+    lax.fori_loop(0, 1, first, 0)
+    for m in range(1, n_pb):
+        to = lax.rem(me + m, n_pb)
+        send(marks_ref.at[me], marks_ref.at[me], msend, mrecv, {"pb": to}).start()
+    lax.fori_loop(1, middle, first, 0)
     if square:
         come(0, 1)
         piece(2, peers[0], 1, hsend, peers[1]).start()
@@ -348,6 +353,9 @@
         for h in range(2):
             come(2, h)
             pass_half(2, h).start()
+    some = marks_ref.at[pl.ds(0, n_pb - 1)]
+    send(some, some, msend, mrecv, {"pb": sibling}).wait_recv()
+    markz_ref[pl.ds(slab, 1)] = jnp.sum(marks_ref[...], 0, keepdims=True)
     table_copy.wait()
 
     def pair_at(line, b):
@@ -368,6 +376,9 @@
     def near_copy(i):
         return send(near_ref.at[i], nearin_ref.at[i], nsend, nrecv.at[i], {"pb": sibling})
 
+    for m in range(1, n_ga):
+        to = lax.rem(slab + m, n_ga)
+        send(markz_ref.at[slab], markz_ref.at[slab], zsend, zrecv, {"ga": to}).start()
     pair = math.gcd(blocks, 4)
     order = list(range(chips - 2, -1, -1)) + [chips - 1]
     for n, i in enumerate(order):
@@ -470,16 +481,27 @@
     tail = hid - channels
     top += exact(acc_ref[channels : 2 * channels], gathered(112))
     rest = exact(acc_ref[2 * channels : 2 * channels + tail], gathered(120))
-    flag = jnp.where(left > 0, 1.0, 0.0)
-    slices = channels // n_pb
     top = jnp.concatenate([top[:tail] + rest, top[tail:]], 0)
-    marked = (lax.rem(rows_of((channels, LANES)), slices) == 0) & (cols_of((channels, LANES)) == LANES - 1)
-    top = jnp.where(marked, flag, top)
-    ar_ref[...] = top.reshape(n_pb, slices, LANES)
-    arin_ref[pl.ds(me, 1)] = ar_ref[pl.ds(me, 1)]
-    for m in range(1, n_pb):
-        to = lax.rem(me + m, n_pb)
-        send(ar_ref.at[to], arin_ref.at[me], asend, arecv, {"pb": to}).start()
+    slices = channels // chips
+    ar_ref[...] = top.reshape(chips, slices, LANES)
+
+    def counted(n, ssem, rsem):
+        some = arin_ref.at[pl.ds(0, n)]
+        return send(some, some, ssem, rsem, {"pb": sibling})
+
+    for m in range(1, chips):
+        to = lax.rem(chip + m, chips)
+        send(ar_ref.at[to], arin_ref.at[me], asend, arecv, {"pb": to * 2 + 1}).start()
+
+    @pl.when(core == 0)
+    def _():
+        send(ar_ref.at[chip], arin_ref.at[me], asend, arecv, {"pb": sibling}).start()
+
+    some = markz_ref.at[pl.ds(0, n_ga - 1)]
+    send(some, some, zsend, zrecv, {"pb": sibling}).wait_recv()
+    more_ref[0] = jnp.max(jnp.sum(markz_ref[...], 0)).astype(I32)
+    tell = pltpu.make_async_copy(more_ref, more_out, out_sem)
+    tell.start()
     if square:
         for copy in early[2:]:
             copy.start()
@@ -487,27 +509,31 @@
             copy.wait_recv()
             into = far_ref.at[1 - i, pl.ds(i * half, half)]
             into[...] = (into[...].astype(F32) + half_ref[i].astype(F32)).astype(BF16)
-    most = pl.ds(0, n_pb - 1)
-    all_in = send(ar_ref.at[most], arin_ref.at[most], asend, arecv, {"pb": sibling})
-    all_in.wait_recv()
-    gaall_ref[pl.ds(slab, 1)] = jnp.sum(arin_ref[...], 0, keepdims=True)
-    for m in range(1, n_ga):
-        to = lax.rem(slab + m, n_ga)
-        send(gaall_ref.at[slab], gaall_ref.at[slab], bsend, brecv, {"ga": to}).start()
+
+    @pl.when(core == 0)
+    def _():
+        counted(chips, asend, arecv).wait_send()
+
+    @pl.when(core == 1)
+    def _():
+        arin_ref[pl.ds(me, 1)] = ar_ref[pl.ds(chip, 1)]
+        counted(n_pb - 1, asend, arecv).wait_recv()
+        gaall_ref[pl.ds(slab, 1)] = jnp.sum(arin_ref[...], 0, keepdims=True)
+        for m in range(1, n_ga):
+            to = lax.rem(slab + m, n_ga)
+            send(gaall_ref.at[slab], gaall_ref.at[slab], bsend, brecv, {"ga": to}).start()
+
     if square:
         for copy in late:
             copy.start()
-    less = gaall_ref.at[pl.ds(0, n_ga - 1)]
-    all_slabs = send(less, less, bsend, brecv, {"pb": sibling})
-    all_slabs.wait_recv()
-    settled = jnp.sum(gaall_ref[...], 0, keepdims=True)
-    fin_ref[pl.ds(me, 1)] = settled
-    more_ref[0] = jnp.sum(jnp.where(cols_of((1, LANES)) == LANES - 1, settled[0, 0:1], 0.0)).astype(I32)
-    for m in range(1, n_pb):
-        to = lax.rem(me + m, n_pb)
-        send(fin_ref.at[me], fin_ref.at[me], csend, crecv, {"pb": to}).start()
-    tell = pltpu.make_async_copy(more_ref, more_out, out_sem)
-    tell.start()
+
+    @pl.when(core == 1)
+    def _():
+        counted(n_ga - 1, bsend, brecv).wait_recv()
+        fin_ref[pl.ds(chip, 1)] = jnp.sum(gaall_ref[...], 0, keepdims=True)
+        for m in range(1, n_pb):
+            to = lax.rem(me + m, n_pb)
+            send(fin_ref.at[chip], fin_ref.at[chip], csend, crecv, {"pb": to}).start()
 
     if square:
         come_in = farin_ref.at[pl.ds(0, 2)]
@@ -521,8 +547,14 @@
             value += farin_ref[i, b].astype(F32)
         grid_ref[0, :, b * LANES : (b + 1) * LANES] = value
 
-    all_final = send(fin_ref.at[most], fin_ref.at[most], csend, crecv, {"pb": sibling})
-    all_final.wait_recv()
+    @pl.when(core == 0)
+    def _():
+        counted(chips, csend, crecv).wait_recv()
+
+    @pl.when(core == 1)
+    def _():
+        counted(chips - 1, csend, crecv).wait_recv()
+
     final = fin_ref[...].reshape(channels, LANES)
     final_ref[...] = final
     tell.wait()
@@ -536,8 +568,17 @@
     else:
         for copy in fars:
             copy.wait_send()
-    for copy in (all_in, all_slabs, all_final):
-        copy.wait_send()
+
+    @pl.when(core == 1)
+    def _():
+        counted(chips - 1, asend, arecv).wait_send()
+        counted(n_ga - 1, bsend, brecv).wait_send()
+        counted(n_pb - 1, csend, crecv).wait_send()
+
+    marks_in = marks_ref.at[pl.ds(0, n_pb - 1)]
+    send(marks_in, marks_in, msend, mrecv, {"pb": sibling}).wait_send()
+    marks_in = markz_ref.at[pl.ds(0, n_ga - 1)]
+    send(marks_in, marks_in, zsend, zrecv, {"pb": sibling}).wait_send()
 
 
 def call(step, collective_id, query_points, cotangent, slab_ids, rel_cells, offsets, latent, w_in, b_in, w_out, b_out):
@@ -553,7 +594,7 @@
     hbm = pl.BlockSpec(memory_space=pltpu.HBM)
     vmem = pl.BlockSpec(memory_space=pltpu.VMEM)
     dma = pltpu.SemaphoreType.DMA
-    slices = channels // n_pb
+    slices = channels // chips
     ins = (offsets, offsets, w_in.T, b_in[None], w_out, b_out[None], slab_ids, query_points, rel_cells, cotangent)
     ins += () if step is None else (step,)
     outs = [
@@ -594,10 +635,12 @@
             pltpu.VMEM((2, max(blocks // 2, 1), channels, LANES), BF16),
             pltpu.VMEM((blocks, channels, LANES), F32),
             pltpu.VMEM((channels + hid, LANES), F32),
-            pltpu.VMEM((n_pb, slices, LANES), F32),
+            pltpu.VMEM((chips, slices, LANES), F32),
             pltpu.VMEM((n_pb, slices, LANES), F32),
             pltpu.VMEM((n_ga, slices, LANES), F32),
-            pltpu.VMEM((n_pb, slices, LANES), F32),
+            pltpu.VMEM((chips, slices, LANES), F32),
+            pltpu.VMEM((n_pb, 8, LANES), F32),
+            pltpu.VMEM((n_ga, 8, LANES), F32),
             dma((len(ins),)),
             dma,
             dma,
@@ -612,6 +655,10 @@
             dma((chips,)),
             dma,
             dma((3,)),
+            dma,
+            dma,
+            dma,
+            dma,
             dma,
             dma,
             dma,

time: 34.8 us -> 34.4 us (0.989)
  Pallas kernels: 33.4 us -> 32.7 us
    pallas_call x1, Pallas kernels: 32.3 us -> 31.6 us  [call(): pl.pallas_call(functools.partial(kernel, n_pb, n_ga, len(ins)), out_shape...]
where the time goes in v6:
time: 34.4 us; the launch traced here: 34.3 us
  Pallas kernels  32.7 us (95%)
  between operations  0.81 us (2%)
  loops' own time  0.75 us (2%)
    pallas_call x1, Pallas kernels, call(): pl.pallas_call(functools.partial(kernel, n_pb, n_ga, len(ins)), out_shape...  31.6 us
    pallas_call x1, Pallas kernels, shards(): pl.pallas_call(functools.partial(settle, float(queries) ** (-0.5)), out_s...  1.14 us
    another operation x1, loops' own time, shards(): grid, final = lax.while_loop(lambda state: state[1][0] > 0, again, first)[2]  0.75 us

profile of v6, /device:TPU:0, one launch (start us, length us, event | category | flops | bytes accessed | tf_op | source)
XLA Modules:
  0.0 34.3 jit_solution(17527125290493300435)
XLA Ops:
  0.6 31.6 %whole.2 = (f32[1,64,2048]{2,1,0:T(8,128)S(1)}, f32[64,128]{1,0:T(8,128)S(1)}, s32[1]{0:T(128)}) custom-call(bf16[1,64,2048]{2,1,0:T(8,128)(2,1)} %latent_in.1, s32[1,32]{1,0:T(1,128)} %rest_1_.1, s32[1,32]{1,0:T(1,128)} %rest_1_.1, f32[6,80]{1,0:T(8,128)} %bitcast.14, f32[1,80]{1,0:T(1,128)} %bitcast.16, bf16[64,80]{1,0:T(8,128)(2,1)} %rest_4_.1, ...), custom_call_target="tpu_custom_call" | custom-call | tf_op jit(solution)/shard_map/whole/pallas_call | solution.py:605
  32.2 0.8 %while.14 = (s32[1]{0:T(128)}, s32[1]{0:T(128)}, f32[1,64,2048]{2,1,0:T(8,128)S(1)}, f32[64,128]{1,0:T(8,128)S(1)}, f32[80,6]{0,1:T(8,128)}, /*index=5*/f32[80]{...) while((s32[1]{0:T(128)}, s32[1]{0:T(128)}, ...), condition=%wide.region_1.0_spmd, body=%wide.region_0.0_spmd | while | flops 139266 | bytes 1802417 | solution.py:713
  33.0 1.1 %settle.1 = (f32[1,64,2048]{2,1,0:T(8,128)}, f32[6,80]{1,0:T(8,128)}, f32[1,80]{1,0:T(1,128)}, f32[64,80]{1,0:T(8,128)}, f32[1,64]{1,0:T(1,128)}) custom-call(f32[1,64,2048]{2,1,0:T(8,128)S(1)} %get-tuple-element.91.grid_in, f32[64,128]{1,0:T(8,128)S(1)} %get-tuple-element.92.final_ref), custom_call_target="tpu_custom_call" | custom-call | tf_op jit(solution)/shard_map/settle/pallas_call | solution.py:719
